TPU v7x, 32 devices: a whole 2x2x4 slice. The times are simulated.
32 devices in a mesh: tp: 4 (over z), dp: 8 (over y, x, core).
Axes of the slice: x: 2, y: 2, z: 4, core: 2. Of those that a mesh axis runs over, the one named last changes fastest.
Arguments:
- x_saved: bfloat16 [8, 768, 4096], P('dp', 'tp')
- dy_out: bfloat16 [8, 768, 4096], P('dp', 'tp')
- ln_params: float32 [4, 4096], replicated
- w_qkv: bfloat16 [4096, 8, 6, 128], P(None, 'tp')
- w_out: bfloat16 [4096, 4096], P('tp')
- w_up: bfloat16 [4096, 16384], P(None, 'tp')
- w_down: bfloat16 [16384, 4096], P('tp')
Outputs:
- output 1: bfloat16 [8, 768, 4096], P('dp', 'tp')
- output 2: float32 [4, 4096], replicated
- output 3: float32 [4096, 8, 6, 128], P('dp', 'tp')
- output 4: float32 [4096, 4096], P(('tp', 'dp'))
- output 5: float32 [4096, 16384], P('dp', 'tp')
- output 6: float32 [16384, 4096], P(('tp', 'dp'))
All inputs are finite; a program needn't handle non-finite values.
Results may differ from a plain program's by a relative error of at most 0.0111644.
Values are sent between devices in bfloat16 or wider.
A program may use at most 1 GiB of HBM per device.

v0:
```python
import jax
import jax.numpy as jnp
from jax import lax
from jax.sharding import PartitionSpec as P

NORM_EPS = 1e-5
ROPE_BASE = 10000.0


def layer_norm(x_rows, norm_gain, norm_shift):
    row_mean = jnp.mean(x_rows, axis=-1, keepdims=True)
    centered = x_rows - row_mean
    row_var = jnp.mean(centered * centered, axis=-1, keepdims=True)
    return (centered * lax.rsqrt(row_var + NORM_EPS) * norm_gain + norm_shift).astype(jnp.bfloat16)


def rope_tables(positions, head_dim):
    half_dim = head_dim // 2
    inv_freq = ROPE_BASE ** (-2.0 * jnp.arange(half_dim, dtype=jnp.float32) / head_dim)
    angles = positions.astype(jnp.float32)[:, None] * inv_freq[None, :]
    return jnp.cos(angles), jnp.sin(angles)


def apply_rope(tensor, cos_t, sin_t):
    half_dim = tensor.shape[-1] // 2
    t_f32 = tensor.astype(jnp.float32)
    lo_half = t_f32[..., :half_dim]
    hi_half = t_f32[..., half_dim:]
    return jnp.concatenate([lo_half * cos_t - hi_half * sin_t, hi_half * cos_t + lo_half * sin_t], axis=-1).astype(jnp.bfloat16)


def gelu_bf16(hidden):
    return jax.nn.gelu(hidden.astype(jnp.float32), approximate=False).astype(jnp.bfloat16)


def attention_core(qkv_proj, cos_t, sin_t):
    q_slots = qkv_proj.shape[3] - 2
    positions = jnp.arange(qkv_proj.shape[1])
    rotated = apply_rope(qkv_proj[:, :, :, :q_slots + 1, :], cos_t[:, None, None, :], sin_t[:, None, None, :])
    query_rot = rotated[:, :, :, :q_slots, :]
    key_rot = rotated[:, :, :, q_slots, :]
    values = qkv_proj[:, :, :, q_slots + 1, :]
    scores = jnp.einsum('btgqh,bsgh->bgqts', query_rot, key_rot, preferred_element_type=jnp.float32) * (qkv_proj.shape[4] ** -0.5)
    causal = positions[:, None] >= positions[None, :]
    attn_probs = jax.nn.softmax(jnp.where(causal, scores, -1e30), axis=-1).astype(jnp.bfloat16)
    return jnp.einsum('bgqts,bsgh->btgqh', attn_probs, values, preferred_element_type=jnp.float32).astype(jnp.bfloat16)


def solution(mesh):
    def local_step(x_loc, dy_loc, ln_params, w_qkv, w_out, w_up, w_down):
        x_full = lax.all_gather(x_loc, 'tp', axis=1, tiled=True)
        x_full_f32 = x_full.astype(jnp.float32)
        h_attn = layer_norm(x_full_f32, ln_params[0], ln_params[1])
        h_mlp = layer_norm(x_full_f32, ln_params[2], ln_params[3])
        qkv_proj = jnp.einsum('btd,dgjh->btgjh', h_attn, w_qkv, preferred_element_type=jnp.float32).astype(jnp.bfloat16)
        cos_t, sin_t = rope_tables(jnp.arange(x_full.shape[1]), w_qkv.shape[3])
        context, attn_pull = jax.vjp(lambda qkv_in: attention_core(qkv_in, cos_t, sin_t), qkv_proj)
        hidden = jnp.einsum('btd,df->btf', h_mlp, w_up, preferred_element_type=jnp.float32).astype(jnp.bfloat16)
        gelu_out, gelu_pull = jax.vjp(gelu_bf16, hidden)
        dy_full = lax.all_gather(dy_loc, 'tp', axis=1, tiled=True)
        num_seqs, seq_len = dy_full.shape[0], dy_full.shape[1]
        d_ctx = jnp.einsum('btd,cd->btc', dy_full, w_out, preferred_element_type=jnp.float32).astype(jnp.bfloat16)
        g_wout = jnp.einsum('btc,btd->cd', context.reshape(num_seqs, seq_len, -1), dy_full, preferred_element_type=jnp.float32)
        (d_proj,) = attn_pull(d_ctx.reshape(context.shape))
        g_wqkv = jnp.einsum('btd,btgjh->dgjh', h_attn, d_proj, preferred_element_type=jnp.float32)
        d_hattn_part = jnp.einsum('btgjh,dgjh->btd', d_proj, w_qkv, preferred_element_type=jnp.float32).astype(jnp.bfloat16)
        d_gelu = jnp.einsum('btd,fd->btf', dy_full, w_down, preferred_element_type=jnp.float32).astype(jnp.bfloat16)
        g_wdown = jnp.einsum('btf,btd->fd', gelu_out, dy_full, preferred_element_type=jnp.float32)
        (d_hidden,) = gelu_pull(d_gelu)
        g_wup = jnp.einsum('btd,btf->df', h_mlp, d_hidden, preferred_element_type=jnp.float32)
        d_hmlp_part = jnp.einsum('btf,df->btd', d_hidden, w_up, preferred_element_type=jnp.float32).astype(jnp.bfloat16)
        d_hattn = lax.psum_scatter(d_hattn_part, 'tp', scatter_dimension=1, tiled=True)
        d_hmlp = lax.psum_scatter(d_hmlp_part, 'tp', scatter_dimension=1, tiled=True)
        x_loc_f32 = x_loc.astype(jnp.float32)
        _, attn_norm_pull = jax.vjp(layer_norm, x_loc_f32, ln_params[0], ln_params[1])
        _, mlp_norm_pull = jax.vjp(layer_norm, x_loc_f32, ln_params[2], ln_params[3])
        dx_attn, dgain_attn, dshift_attn = attn_norm_pull(d_hattn)
        dx_mlp, dgain_mlp, dshift_mlp = mlp_norm_pull(d_hmlp)
        grad_x = (dy_loc.astype(jnp.float32) + dx_attn + dx_mlp).astype(jnp.bfloat16)
        grad_ln = lax.psum(jnp.stack([dgain_attn, dshift_attn, dgain_mlp, dshift_mlp]), ('tp', 'dp'))
        grad_wqkv = lax.psum_scatter(g_wqkv, 'dp', scatter_dimension=0, tiled=True)
        grad_wout = lax.psum_scatter(g_wout, 'dp', scatter_dimension=0, tiled=True)
        grad_wup = lax.psum_scatter(g_wup, 'dp', scatter_dimension=0, tiled=True)
        grad_wdown = lax.psum_scatter(g_wdown, 'dp', scatter_dimension=0, tiled=True)
        return grad_x, grad_ln, grad_wqkv, grad_wout, grad_wup, grad_wdown

    act_spec = P('dp', 'tp', None)
    in_specs = (act_spec, act_spec, P(None, None), P(None, 'tp', None, None), P('tp', None), P(None, 'tp'), P('tp', None))
    out_specs = (act_spec, P(None, None), P('dp', 'tp', None, None), P(('tp', 'dp'), None), P('dp', 'tp'), P(('tp', 'dp'), None))
    return jax.shard_map(local_step, mesh=mesh, in_specs=in_specs, out_specs=out_specs, check_vma=False)
```

profile of v0, /device:TPU:0, one launch (start us, length us, event | category | flops | bytes accessed | tf_op | source)
XLA Modules:
  0.0 1800.8 jit_solution(2896287705542168415)
XLA Ops:
  7.2 0.7 all-gather.5.cloned.1.call-update
  7.9 0.7 all-gather.3.cloned.1.call-update
  8.7 31.1 %copy.14 = bf16[4096,2,6,128]{0,3,2,1:T(8,128)(2,1)} copy(bf16[4096,2,6,128]{3,1,2,0:T(2,128)(2,1)} %param.10) | data formatting | bytes 25165824 | tf_op args[3]
  39.9 1.0 iota_compare_fusion
  40.9 1.5 multiply_cosine_fusion
  42.4 0.7 fusion.154
  43.0 84.2 %all-gather.5.cloned.1.call-done = bf16[1,768,4096]{2,1,0:T(8,128)(2,1)} async-done(((bf16[1,192,4096]{2,1,0:T(8,128)(2,1)}), bf16[1,768,4096]{2,1,0:T(8,128)(2,1)}) %all-gather.5.cloned.1.call-update) | async-done | bytes 6291472 | tf_op jit(solution)/shard_map/all_gather | solution.py:51
  127.2 3.7 convert_reduce_fusion
  130.9 4.5 fusion.20
  135.5 106.7 %all-gather.3.cloned.1.call-done = bf16[1,768,4096]{2,1,0:T(8,128)(2,1)} async-done(((bf16[1,192,4096]{2,1,0:T(8,128)(2,1)}), bf16[1,768,4096]{2,1,0:T(8,128)(2,1)}) %all-gather.3.cloned.1.call-update) | async-done | bytes 6291472 | tf_op jit(solution)/shard_map/all_gather | solution.py:60
  242.2 11.0 fusion.103
  253.2 1.6 copy.38
  254.8 32.4 %convolution_convert_fusion.2 = bf16[768,4096]{1,0:T(8,128)(2,1)S(1)} fusion(bf16[4096,4096]{1,0:T(8,128)(2,1)} %param.12, bf16[1,768,4096]{2,1,0:T(8,128)(2,1)} %all-gather.5.cloned.1.call-done, f32[4096]{0:T(1024)S(1)} %bitcast.237, f32[4096]{0:T(1024)S(1)} %bitcast.223, f32[768]{0:T(1024)S(1)} %add_rsqrt_fusion, f32[768]{0:T(1024)S(1)} %broadcast_multiply_fusion), kind=kOutput, calls=%fused_computation.76 | convolution fusion | flops 25791823872 | bytes 46176256 | tf_op jit(solution)/shard_map/btd,df->btf/dot_general | solution.py:58
  287.2 2.7 copy-done.32
  289.9 59.2 %fusion.55 = bf16[768,4096]{1,0:T(8,128)(2,1)S(1)} fusion(bf16[768,4096]{1,0:T(8,128)(2,1)S(1)} %convolution_convert_fusion.2, bf16[4096,4096]{1,0:T(8,128)(2,1)} %param.13, bf16[1,768,4096]{2,1,0:T(8,128)(2,1)} %all-gather.3.cloned.1.call-done), kind=kOutput, calls=%fused_computation.67 | convolution fusion | flops 26005733376 | bytes 52428800 | tf_op jit(solution)/shard_map/btd,fd->btf/dot_general | solution.py:67
  349.1 2.6 copy-done.31
  351.7 31.9 %fusion.79 = bf16[1,768,4096]{2,1,0:T(8,128)(2,1)} fusion(bf16[768,4096]{1,0:T(8,128)(2,1)S(1)} %fusion.55, bf16[4096,4096]{1,0:T(8,128)(2,1)} %param.12), kind=kOutput, calls=%fused_computation.92 | convolution fusion | flops 25772949504 | bytes 46137344 | tf_op jit(solution)/shard_map/btf,df->btd/dot_general | solution.py:71
  383.7 15.2 fusion.66
  399.9 0.6 subtract_convert_fusion
  400.6 8.3 fusion.9
  408.9 10.2 fusion.134
  419.1 12.7 fusion.8
  431.8 13.5 fusion.110
  445.4 13.5 fusion.128
  459.1 0.5 multiply_add_fusion.1
  460.2 11.3 fusion.125
  471.6 13.3 fusion.80
  485.0 16.8 fusion.64
  501.8 1.3 copy-done
  503.5 10.6 fusion.106
  514.1 92.8 %reduce-scatter.7.cloned.1.call-done = bf16[1,192,4096]{2,1,0:T(8,128)(2,1)} async-done(((bf16[1,768,4096]{2,1,0:T(8,128)(2,1)}), bf16[1,192,4096]{2,1,0:T(8,128)(2,1)}) %reduce-scatter.7.cloned.1.call-update) | async-done | bytes 1572880 | tf_op jit(solution)/shard_map/reduce_scatter | solution.py:72
  606.9 3.7 fusion.92
  610.7 4.9 fusion.94
  615.6 0.7 pad_maximum_fusion.1
  616.3 12.5 fusion.69
  628.9 0.6 copy-done.17
  629.6 39.4 %fusion.148 = f32[4096,4096]{1,0:T(8,128)} fusion(bf16[768,4096]{1,0:T(8,128)(2,1)} %copy-done.31, bf16[1,768,4096]{2,1,0:T(8,128)(2,1)} %all-gather.5.cloned.1.call-done, f32[4096]{0:T(1024)S(1)} %bitcast.238, f32[4096]{0:T(1024)S(1)} %bitcast.226, f32[768]{0:T(1024)S(1)} %copy-done.30, f32[768]{0:T(1024)S(1)} %copy-done.15), kind=kOutput, calls=%fused_computation.177 | convolution fusion | flops 25788678144 | bytes 79730688 | tf_op jit(solution)/shard_map/btd,btf->df/dot_general | solution.py:70
  669.1 61.6 %fusion.61 = f32[4096,4096]{1,0:T(8,128)} fusion(bf16[768,4096]{1,0:T(8,128)(2,1)} %copy-done.32, bf16[1,768,4096]{2,1,0:T(8,128)(2,1)} %all-gather.3.cloned.1.call-done), kind=kOutput, calls=%fused_computation.77 | convolution fusion | flops 25977421824 | bytes 79691776 | tf_op jit(solution)/shard_map/btf,btd->fd/dot_general | solution.py:68
  730.8 0.6 copy-done.27
  731.4 0.7 copy-done.1
  732.6 4.7 add_convert_fusion.1
  737.3 28.6 %reduce-scatter.11.cloned.1.call-done = f32[512,2,6,128]{3,0,2,1:T(8,128)} async-done(((f32[4096,2,6,128]{3,0,2,1:T(8,128)}), f32[512,2,6,128]{3,0,2,1:T(8,128)}) %reduce-scatter.11.cloned.1.call-update) | async-done | bytes 3145744 | tf_op jit(solution)/shard_map/reduce_scatter | solution.py:81
  765.9 6.0 copy.24
  771.9 127.5 %all-reduce.8.cloned.1.call-done = f32[4,4096]{1,0:T(4,128)} async-done(((f32[4,4096]{1,0:T(4,128)}), f32[4,4096]{1,0:T(4,128)}) %all-reduce.8.cloned.1.call-update) | async-done | bytes 65552 | tf_op jit(solution)/shard_map/psum | solution.py:80
  899.4 118.5 %reduce-scatter.13.cloned.1.call-done = f32[128,4096]{1,0:T(8,128)} async-done(((f32[1024,4096]{1,0:T(8,128)}), f32[128,4096]{1,0:T(8,128)}) %reduce-scatter.13.cloned.1.call-update) | async-done | bytes 2097168 | tf_op jit(solution)/shard_map/reduce_scatter | solution.py:82
  1017.9 387.2 %reduce-scatter.15.cloned.1.call-done = f32[512,4096]{1,0:T(8,128)} async-done(((f32[4096,4096]{1,0:T(8,128)}), f32[512,4096]{1,0:T(8,128)}) %reduce-scatter.15.cloned.1.call-update) | async-done | bytes 8388624 | tf_op jit(solution)/shard_map/reduce_scatter | solution.py:83
  1405.1 387.2 %reduce-scatter.17.cloned.1.call-done = f32[512,4096]{1,0:T(8,128)} async-done(((f32[4096,4096]{1,0:T(8,128)}), f32[512,4096]{1,0:T(8,128)}) %reduce-scatter.17.cloned.1.call-update) | async-done | bytes 8388624 | tf_op jit(solution)/shard_map/reduce_scatter | solution.py:84
  1792.3 1.5 copy.45
  (99 shorter events, 3.3 us)
Async XLA Ops:
  7.2 120.0 %all-gather.5.cloned.1.call-start = ((), (), s32[]{:S(2)}) async-start(), calls=%async_computation.7 | async-start | bytes 7864320 | tf_op jit(solution)/shard_map/all_gather | solution.py:51
  7.9 234.3 %all-gather.3.cloned.1.call-start = ((), (), s32[]{:S(2)}) async-start(), calls=%async_computation.6 | async-start | bytes 7864320 | tf_op jit(solution)/shard_map/all_gather | solution.py:60
  8.6 33.7 %copy-start.13 = (f32[4,4096]{1,0:T(4,128)S(1)}, f32[4,4096]{1,0:T(4,128)}, u32[]{:S(2)}) copy-start(f32[4,4096]{1,0:T(4,128)} %param.9) | copy-start | bytes 196612
  8.7 505.4 %reduce-scatter.9.cloned.1.call-start = ((), (), s32[]{:S(2)}) async-start(), calls=%async_computation.9 | async-start | bytes 7864320 | tf_op jit(solution)/shard_map/reduce_scatter | solution.py:73
  43.0 211.7 %copy-start.9 = (f32[1,4096]{1,0:T(1,128)}, f32[1,4096]{1,0:T(1,128)S(1)}, u32[]{:S(2)}) copy-start(f32[1,4096]{1,0:T(1,128)S(1)} %get-tuple-element.29) | copy-start | bytes 49156
  43.0 211.7 %copy-start.16 = (f32[1,4096]{1,0:T(1,128)}, f32[1,4096]{1,0:T(1,128)S(1)}, u32[]{:S(2)}) copy-start(f32[1,4096]{1,0:T(1,128)S(1)} %get-tuple-element.32) | copy-start | bytes 49156
  130.9 123.9 %copy-start.14 = (f32[768]{0:T(1024)}, f32[768]{0:T(1024)S(1)}, u32[]{:S(2)}) copy-start(f32[768]{0:T(1024)S(1)} %broadcast_multiply_fusion) | copy-start | bytes 9220
  135.5 119.3 %copy-start.29 = (f32[768]{0:T(1024)}, f32[768]{0:T(1024)S(1)}, u32[]{:S(2)}) copy-start(f32[768]{0:T(1024)S(1)} %add_rsqrt_fusion) | copy-start | bytes 9220
  287.2 2.7 copy-start.32
  349.0 2.6 copy-start.31
  351.7 32.0 %copy-start.11 = (f32[1,4096]{1,0:T(1,128)S(1)}, f32[1,4096]{1,0:T(1,128)}, u32[]{:S(2)}) copy-start(f32[1,4096]{1,0:T(1,128)} %get-tuple-element.31) | copy-start | bytes 49156
  351.7 32.0 %copy-start.15 = (f32[768]{0:T(1024)S(1)}, f32[768]{0:T(1024)}, u32[]{:S(2)}) copy-start(f32[768]{0:T(1024)} %copy-done.14) | copy-start | bytes 9220
  351.7 32.0 %copy-start.18 = (f32[1,4096]{1,0:T(1,128)S(1)}, f32[1,4096]{1,0:T(1,128)}, u32[]{:S(2)}) copy-start(f32[1,4096]{1,0:T(1,128)} %get-tuple-element.30) | copy-start | bytes 49156
  351.7 32.0 %copy-start.30 = (f32[768]{0:T(1024)S(1)}, f32[768]{0:T(1024)}, u32[]{:S(2)}) copy-start(f32[768]{0:T(1024)} %copy-done.29) | copy-start | bytes 9220
  383.6 223.3 %reduce-scatter.7.cloned.1.call-start = ((), (), s32[]{:S(2)}) async-start(), calls=%async_computation.8 | async-start | bytes 7864320 | tf_op jit(solution)/shard_map/reduce_scatter | solution.py:72
  398.9 0.9 copy-start.6
  398.9 1.0 copy-start.7
  398.9 1.7 copy-start.3
  399.2 1.4 copy-start.4
  458.8 1.4 copy-start.8
  459.6 12.0 slice-start
  460.2 11.4 copy-start.5
  460.2 11.4 slice-start.1
  460.2 11.4 slice-start.2
  484.9 281.0 %reduce-scatter.11.cloned.1.call-start = ((), (), s32[]{:S(2)}) async-start(), calls=%async_computation.11 | async-start | bytes 28311552 | tf_op jit(solution)/shard_map/reduce_scatter | solution.py:81
  501.7 1.4 copy-start
  501.8 397.6 %all-reduce.8.cloned.1.call-start = ((), (), s32[]{:S(2)}) async-start(), calls=%async_computation.10 | async-start | bytes 131072 | tf_op jit(solution)/shard_map/psum | solution.py:80
  503.5 107.2 %copy-start.19 = (f32[192]{0:T(256)}, f32[192]{0:T(256)S(1)}, u32[]{:S(2)}) copy-start(f32[192]{0:T(256)S(1)} %broadcast_multiply_fusion.1) | copy-start | bytes 2308
  503.5 103.4 %copy-start.10 = (f32[1,4096]{1,0:T(1,128)S(1)}, f32[1,4096]{1,0:T(1,128)}, u32[]{:S(2)}) copy-start(f32[1,4096]{1,0:T(1,128)} %copy-done.9) | copy-start | bytes 49156
  610.6 18.2 %copy-start.21 = (f32[192]{0:T(256)}, f32[192]{0:T(256)S(1)}, u32[]{:S(2)}) copy-start(f32[192]{0:T(256)S(1)} %get-tuple-element.23) | copy-start | bytes 2308
  610.6 18.2 %copy-start.23 = (f32[192]{0:T(256)}, f32[192]{0:T(256)S(1)}, u32[]{:S(2)}) copy-start(f32[192]{0:T(256)S(1)} %get-tuple-element.35) | copy-start | bytes 2308
  610.6 18.2 %copy-start.25 = (f32[192]{0:T(256)}, f32[192]{0:T(256)S(1)}, u32[]{:S(2)}) copy-start(f32[192]{0:T(256)S(1)} %multiply_multiply_fusion.1) | copy-start | bytes 2308
  616.3 401.6 %reduce-scatter.13.cloned.1.call-start = ((), (), s32[]{:S(2)}) async-start(), calls=%async_computation.12 | async-start | bytes 18874368 | tf_op jit(solution)/shard_map/reduce_scatter | solution.py:82
  628.9 0.7 copy-start.17
  628.9 776.2 %reduce-scatter.15.cloned.1.call-start = ((), (), s32[]{:S(2)}) async-start(), calls=%async_computation.13 | async-start | bytes 75497472 | tf_op jit(solution)/shard_map/reduce_scatter | solution.py:83
  669.0 1123.3 %reduce-scatter.17.cloned.1.call-start = ((), (), s32[]{:S(2)}) async-start(), calls=%async_computation.14 | async-start | bytes 75497472 | tf_op jit(solution)/shard_map/reduce_scatter | solution.py:84
  730.7 0.7 copy-start.27
  730.7 0.7 copy-start.28
  730.7 1.4 copy-start.1
  730.7 1.9 copy-start.2
  730.7 1.9 copy-start.12
  730.7 1.9 copy-start.20
  730.7 1.9 copy-start.22
  730.7 1.8 copy-start.24
  730.8 1.8 copy-start.26
Sparse Core Ops, SparseCore 0:
  9.5 117.6 all-gather.4
  128.8 113.3 all-gather.2
  383.7 109.0 reduce-scatter.8
  495.6 111.2 reduce-scatter.6
  610.4 155.5 reduce-scatter.10
  771.9 127.4 all-reduce.7
  903.5 114.3 reduce-scatter.12
  1022.0 383.0 reduce-scatter.14
  1409.2 383.0 reduce-scatter.16
where the time goes:
time: 1810 us; the launch traced here: 1800 us
  waiting for transfers between devices  1330 us (73%)
  matrix products  363 us (20%)
  local copies, waits for them, and re-layouts  50.8 us (3%)
  other arithmetic  37.6 us (2%)
    reduce_scatter x1, waiting for transfers between devices, local_step(): lax.psum_scatter(g_wdown, 'dp', scatter_dimension=0, tiled=True)  387 us
    reduce_scatter x1, waiting for transfers between devices, local_step(): grad_wup = lax.psum_scatter(g_wup, 'dp', scatter_dimension=0, tiled=True)  387 us
    psum x1, waiting for transfers between devices, local_step(): lax.psum(jnp.stack([dgain_attn, dshift_attn, dgain_mlp, dshift_mlp]), ('t...  127 us
    reduce_scatter x1, waiting for transfers between devices, local_step(): grad_wout = lax.psum_scatter(g_wout, 'dp', scatter_dimension=0, tiled=True)  118 us
    all_gather x1, waiting for transfers between devices, local_step(): dy_full = lax.all_gather(dy_loc, 'tp', axis=1, tiled=True)  107 us
    reduce_scatter x1, waiting for transfers between devices, local_step(): lax.psum_scatter(d_hattn_part, 'tp', scatter_dimension=1, tiled=True)  92.8 us
    all_gather x1, waiting for transfers between devices, local_step(): x_full = lax.all_gather(x_loc, 'tp', axis=1, tiled=True)  84.2 us
    dot_general x1, matrix products, local_step(): jnp.einsum('btf,btd->fd', gelu_out, dy_full, preferred_element_type=jnp.f...  61.6 us
  transfers between devices with their start and end apart: 9, of which 8 were waited for; matrix products, arithmetic and copies ran while one was open for 17% of the time, Pallas kernels for 0%

commit v1 on v0

v1 whole, which is shorter than its diff:
```python
import jax
import jax.numpy as jnp
from jax import lax
from jax.sharding import PartitionSpec as P

NORM_EPS = 1e-5
ROPE_BASE = 10000.0
CORE, XAX, YAX = 1, 2, 4
F32, BF16 = jnp.float32, jnp.bfloat16


def norm_stats(x_rows):
    row_mean = jnp.mean(x_rows, axis=-1, keepdims=True)
    centered = x_rows - row_mean
    row_var = jnp.mean(centered * centered, axis=-1, keepdims=True)
    return row_mean, lax.rsqrt(row_var + NORM_EPS)


def norm_apply(x_rows, row_mean, row_rstd, norm_gain, norm_shift):
    return ((x_rows.astype(F32) - row_mean) * row_rstd * norm_gain + norm_shift).astype(BF16)


def layer_norm(x_rows, norm_gain, norm_shift):
    row_mean, row_rstd = norm_stats(x_rows)
    return norm_apply(x_rows, row_mean, row_rstd, norm_gain, norm_shift)


def rope_tables(positions, head_dim):
    half_dim = head_dim // 2
    inv_freq = ROPE_BASE ** (-2.0 * jnp.arange(half_dim, dtype=F32) / head_dim)
    angles = positions.astype(F32)[:, None] * inv_freq[None, :]
    return jnp.cos(angles), jnp.sin(angles)


def apply_rope(tensor, cos_t, sin_t):
    half_dim = tensor.shape[-1] // 2
    t_f32 = tensor.astype(F32)
    lo_half = t_f32[..., :half_dim]
    hi_half = t_f32[..., half_dim:]
    return jnp.concatenate([lo_half * cos_t - hi_half * sin_t, hi_half * cos_t + lo_half * sin_t], axis=-1).astype(BF16)


def attention_core(qkv_proj, cos_t, sin_t):
    q_slots = qkv_proj.shape[3] - 2
    positions = jnp.arange(qkv_proj.shape[1])
    rotated = apply_rope(qkv_proj[:, :, :, :q_slots + 1, :], cos_t[:, None, None, :], sin_t[:, None, None, :])
    query_rot = rotated[:, :, :, :q_slots, :]
    key_rot = rotated[:, :, :, q_slots, :]
    values = qkv_proj[:, :, :, q_slots + 1, :]
    scores = jnp.einsum('btgqh,bsgh->bgqts', query_rot, key_rot, preferred_element_type=F32) * (qkv_proj.shape[4] ** -0.5)
    causal = positions[:, None] >= positions[None, :]
    attn_probs = jax.nn.softmax(jnp.where(causal, scores, -1e30), axis=-1).astype(BF16)
    return jnp.einsum('bgqts,bsgh->btgqh', attn_probs, values, preferred_element_type=F32).astype(BF16)


def swap(value, bit):
    return lax.ppermute(value, 'dp', [(i, i ^ bit) for i in range(8)])


def swap_tp(value, bit):
    return lax.ppermute(value, 'tp', [(i, i ^ bit) for i in range(4)])


def hold(*values):
    return lax.optimization_barrier(values)


def mm(spec, lhs, rhs):
    return jnp.einsum(spec, lhs, rhs, preferred_element_type=F32)


def solution(mesh):
    def local_body(x_in, dy_in, ln_params, w_qkv, w_out, w_up, w_down):
        x_loc, dy_loc = x_in[0], dy_in[0]
        me = lax.axis_index('dp')
        my_c, my_x, my_y = me % 2, (me // 2) % 2, me // 4

        def shares_x(arr, x_at, c_at):
            width = arr.shape[1] // 8
            pick = lambda y: lax.dynamic_slice_in_dim(arr, (y * 4 + x_at * 2 + c_at) * width, width, 1)
            return jnp.concatenate([pick(my_y), pick(1 - my_y)], axis=1)

        def shares_y(arr, y_at, c_at):
            width = arr.shape[1] // 8
            pick = lambda x: lax.dynamic_slice_in_dim(arr, (y_at * 4 + x * 2 + c_at) * width, width, 1)
            return jnp.concatenate([pick(my_x), pick(1 - my_x)], axis=1)

        def spread_x(arr):
            return [shares_x(arr, my_x, my_c), swap(shares_x(arr, my_x, 1 - my_c), CORE),
                    swap(shares_x(arr, 1 - my_x, my_c), XAX),
                    swap(shares_x(arr, 1 - my_x, 1 - my_c), XAX | CORE)]

        def spread_y(arr):
            return [shares_y(arr, my_y, my_c), swap(shares_y(arr, my_y, 1 - my_c), CORE),
                    swap(shares_y(arr, 1 - my_y, my_c), YAX),
                    swap(shares_y(arr, 1 - my_y, 1 - my_c), YAX | CORE)]

        def halves(parts):
            half = parts[0].shape[1] // 2
            return jnp.concatenate([p[:, :half] for p in parts]), jnp.concatenate([p[:, half:] for p in parts])

        def stack4(arr, far):
            return jnp.concatenate([arr, swap(arr, CORE), far, swap(far, CORE)], axis=0)

        x_full = lax.all_gather(x_loc, 'tp', axis=0, tiled=True)
        dy_all = lax.all_gather(dy_loc, 'tp', axis=0, tiled=True)
        seq_len, d_model = x_full.shape
        ff = w_up.shape[1]
        row_mean, row_rstd = norm_stats(x_full.astype(F32))
        h_mlp = norm_apply(x_full, row_mean, row_rstd, ln_params[2], ln_params[3])

        stats = jnp.concatenate([row_mean, row_rstd], axis=1)
        stats4 = jnp.concatenate([stats, swap(stats, CORE), swap(stats, XAX), swap(stats, XAX | CORE)], axis=0)
        x_parts = spread_x(x_full)
        ln_cols = shares_x(ln_params, my_x, my_c)

        h_mlp, _ = hold(h_mlp, x_parts[0])
        hidden, = hold(mm('td,df->tf', h_mlp, w_up).astype(BF16))
        h32 = hidden.astype(F32)
        cdf = 0.5 * (1.0 + lax.erf(h32 * (0.5 ** 0.5)))
        gelu_out, slope = hold((h32 * cdf).astype(BF16), cdf + h32 * (jnp.exp(-0.5 * h32 * h32) * 0.3989422804014327))
        gelu_parts = spread_y(gelu_out)

        x_again, gelu_parts[0] = hold(x_full, gelu_parts[0])
        h_attn = norm_apply(x_again, row_mean, row_rstd, ln_params[0], ln_params[1])
        qkv_proj = jnp.einsum('td,dgjh->tgjh', h_attn, w_qkv, preferred_element_type=F32).astype(BF16)[None]
        cos_t, sin_t = rope_tables(jnp.arange(seq_len), w_qkv.shape[3])
        context, attn_pull = jax.vjp(lambda qkv_in: attention_core(qkv_in, cos_t, sin_t), qkv_proj)
        ctx_parts = spread_y(context.reshape(seq_len, -1))
        mid = d_model // 2
        x_keep, x_send = halves(x_parts)
        norm4 = lambda rows, row, cols: norm_apply(rows, stats4[:, :1], stats4[:, 1:], ln_cols[row, cols], ln_cols[row + 1, cols])
        lo, hi = slice(0, x_keep.shape[1]), slice(x_keep.shape[1], None)
        ha_send, hm_send, ha_keep, hm_keep = hold(
            norm4(x_send, 0, hi), norm4(x_send, 2, hi), norm4(x_keep, 0, lo), norm4(x_keep, 2, lo))

        dy_full, tied = dy_all, dy_all
        dy_lo, dy_hi = hold(dy_full[:, :mid], dy_full[:, mid:])
        far_lo, far_hi = swap(dy_lo, YAX), swap(dy_hi, YAX)
        d_hidden, far_hidden = [], []
        for i in (0, 1):
            cols = slice(i * ff // 2, (i + 1) * ff // 2)
            d_gelu = mm('td,fd->tf', tied, w_down[cols]).astype(BF16)
            d_hid, = hold((d_gelu.astype(F32) * slope[:, cols]).astype(BF16))
            d_hidden.append(d_hid)
            far_hidden.append(swap(d_hid, XAX))
            tied, _ = hold(dy_full, d_hid)

        d_ctx = mm('td,cd->tc', tied, w_out).astype(BF16)
        (d_proj,) = attn_pull(d_ctx.reshape(context.shape))
        d_flat, = hold(d_proj.reshape(seq_len, -1))
        far_proj = swap(d_flat, XAX)
        d_hattn_part, = hold(mm('tk,dk->td', d_flat, w_qkv.reshape(d_model, -1)).astype(BF16))
        d_hattn = lax.psum_scatter(d_hattn_part, 'tp', scatter_dimension=0, tiled=True)
        gelu_keep, gelu_send = halves(gelu_parts)
        ctx_keep, ctx_send = halves(ctx_parts)

        grad = lambda lhs4, rhs4: hold(mm('tr,tc->rc', lhs4, rhs4))[0]
        after = lambda value, *earlier: hold(value, *earlier)[0]
        up4_0 = stack4(d_hidden[0], far_hidden[0])
        up0 = grad(after(hm_send, d_hattn_part), up4_0)
        came_up0 = swap(up0, YAX)
        dy4_0 = stack4(dy_lo, far_lo)
        hid_cat = jnp.concatenate(d_hidden, axis=1)
        d_hmlp_part, = hold(mm('tf,df->td', hid_cat, w_up).astype(BF16))
        d_hmlp = lax.psum_scatter(d_hmlp_part, 'tp', scatter_dimension=0, tiled=True)
        down0 = grad(gelu_send, dy4_0)
        came_down0 = swap(down0, XAX)
        up4_1 = stack4(d_hidden[1], after(far_hidden[1], down0))
        up1 = grad(after(hm_send, down0), up4_1)
        came_up1 = swap(up1, YAX)
        dy4_1 = stack4(dy_hi, after(far_hi, d_hmlp_part))
        down1 = grad(after(gelu_send, up1), dy4_1)
        came_down1 = swap(down1, XAX)
        qkv4 = stack4(d_flat, after(far_proj, down1))
        out0 = grad(after(ctx_send, down1), dy4_0)
        out1 = grad(after(ctx_send, out0), dy4_1)
        came_out = [swap(out0, XAX), swap(out1, XAX)]
        qkv0 = grad(after(ha_send, out1), qkv4)
        came_qkv = swap(qkv0, YAX)
        hm_keep, gelu_keep, ctx_keep, ha_keep, _ = hold(hm_keep, gelu_keep, ctx_keep, ha_keep, qkv0)
        kept_up = [grad(hm_keep, up4_0), grad(hm_keep, up4_1)]
        kept_down = [grad(gelu_keep, dy4_0), grad(gelu_keep, dy4_1)]
        kept_out = [grad(ctx_keep, dy4_0), grad(ctx_keep, dy4_1)]
        kept_qkv = grad(ha_keep, qkv4)
        d_hattn, d_hmlp = after(d_hattn, *kept_up, *kept_down), after(d_hmlp, *kept_up, *kept_down)

        x_loc_f32 = x_loc.astype(F32)
        _, attn_norm_pull = jax.vjp(layer_norm, x_loc_f32, ln_params[0], ln_params[1])
        _, mlp_norm_pull = jax.vjp(layer_norm, x_loc_f32, ln_params[2], ln_params[3])
        dx_attn, dgain_attn, dshift_attn = attn_norm_pull(d_hattn)
        dx_mlp, dgain_mlp, dshift_mlp = mlp_norm_pull(d_hmlp)
        grad_x = (dy_loc.astype(F32) + dx_attn + dx_mlp).astype(BF16)[None]
        grad_ln = jnp.stack([dgain_attn, dshift_attn, dgain_mlp, dshift_mlp])
        for bit in (1, 2):
            grad_ln = grad_ln + swap_tp(grad_ln, bit)
        grad_ln = grad_ln + swap(grad_ln, CORE)
        (kept_up[0], kept_up[1], kept_down[0], kept_down[1], kept_out[0], kept_out[1], kept_qkv, grad_x, grad_ln) = hold(
            *kept_up, *kept_down, *kept_out, kept_qkv, grad_x, grad_ln)
        for bit in (YAX, XAX):
            grad_ln = grad_ln + swap(grad_ln, bit)

        join = lambda kept, came: jnp.concatenate([k + c for k, c in zip(kept, came)], axis=1)
        grad_wqkv = (kept_qkv + came_qkv).reshape((-1,) + w_qkv.shape[1:])
        grad_wup = join(kept_up, (came_up0, came_up1))
        grad_wdown = join(kept_down, (came_down0, came_down1))
        return grad_x, grad_ln, grad_wqkv, join(kept_out, came_out), grad_wup, grad_wdown

    act_spec = P('dp', 'tp', None)
    in_specs = (act_spec, act_spec, P(None, None), P(None, 'tp', None, None), P('tp', None), P(None, 'tp'), P('tp', None))
    out_specs = (act_spec, P(None, None), P('dp', 'tp', None, None), P(('tp', 'dp'), None), P('dp', 'tp'), P(('tp', 'dp'), None))
    return jax.shard_map(local_body, mesh=mesh, in_specs=in_specs, out_specs=out_specs, check_vma=False)
```

time: 1810 us -> 1140 us (0.63)
  waiting for transfers between devices: 1330 us -> 526 us
  other arithmetic: 37.6 us -> 114 us
  local copies, waits for them, and re-layouts: 50.8 us -> 95.8 us
  starting transfers between devices: 0.36 us -> 23.9 us
    reduce_scatter x6 -> x2, waiting for transfers between devices: 1010 us -> 0.01 us  [the longest x1 0.01 us: local_body(): lax.psum_scatter(d_hmlp_part, 'tp', scatter_dimension=0, tiled=True)]
    ppermute x0 -> x39, waiting for transfers between devices: none -> 373 us  [the longest x37 365 us: swap(): return lax.ppermute(value, 'dp', [(i, i ^ bit) for i in range(8)])]
    psum x1 -> x0, waiting for transfers between devices: 127 us -> none  [local_step(): lax.psum(jnp.stack([dgain_attn, dshift_attn, dgain_mlp, dshift_mlp]), ('t...]
    all_gather x2, waiting for transfers between devices: 191 us -> 152 us  [the longest x1 80.2 us: local_body(): x_full = lax.all_gather(x_loc, 'tp', axis=0, tiled=True)]
    add x0 -> x13, other arithmetic: none -> 27.3 us  [the longest x6 13.6 us: local_body(): k + c]
    concatenate x0 -> x19, other arithmetic: none -> 26.9 us  [the longest x3 11.9 us: local_body(): jnp.concatenate([k + c for k, c in zip(kept, came)], axis=1)]
    ppermute x0 -> x39, starting transfers between devices: none -> 23.8 us  [the longest x37 22.6 us: swap(): return lax.ppermute(value, 'dp', [(i, i ^ bit) for i in range(8)])]
    slice x1 -> x14, local copies, waits for them, and re-layouts: 0.65 us -> 24.2 us  [the longest x7 8.18 us: halves(): p[:, half:]]
  transfers between devices with their start and end apart: 9 -> 43, of which waited for: 8 -> 17; matrix products, arithmetic and copies ran while one was open for 17% -> 48% of each run, Pallas kernels for 0% -> 0%
where the time goes in v1:
time: 1140 us; the launch traced here: 1130 us
  waiting for transfers between devices  526 us (46%)
  matrix products  354 us (31%)
  other arithmetic  114 us (10%)
  local copies, waits for them, and re-layouts  95.8 us (8%)
  starting transfers between devices  23.9 us (2%)
  between operations  15.5 us (1%)
    ppermute x37, waiting for transfers between devices, swap(): return lax.ppermute(value, 'dp', [(i, i ^ bit) for i in range(8)])  365 us
    dot_general x20, matrix products, mm(): return jnp.einsum(spec, lhs, rhs, preferred_element_type=F32)  269 us
    all_gather x1, waiting for transfers between devices, local_body(): x_full = lax.all_gather(x_loc, 'tp', axis=0, tiled=True)  80.2 us
    all_gather x1, waiting for transfers between devices, local_body(): dy_all = lax.all_gather(dy_loc, 'tp', axis=0, tiled=True)  71.6 us
    unnamed x199, local copies, waits for them, and re-layouts  55.6 us
    dot_general x3, matrix products, attention_core(): jnp.einsum('btgqh,bsgh->bgqts', query_rot, key_rot, preferred_element_typ...  35.8 us
    dot_general x3, matrix products, attention_core(): jnp.einsum('bgqts,bsgh->btgqh', attn_probs, values, preferred_element_typ...  33.8 us
  transfers between devices with their start and end apart: 43, of which 17 were waited for; matrix products, arithmetic and copies ran while one was open for 48% of the time, Pallas kernels for 0%

profile of v1, /device:TPU:0, one launch (start us, length us, event | category | flops | bytes accessed | tf_op | source)
XLA Modules:
  0.0 1129.3 jit_solution(4493736651379477089)
XLA Ops:
  12.7 31.3 %copy.21 = bf16[4096,2,6,128]{0,3,2,1:T(8,128)(2,1)} copy(bf16[4096,2,6,128]{3,1,2,0:T(2,128)(2,1)} %param.10) | data formatting | bytes 25165824 | tf_op args[3]
  47.5 80.2 %all-gather.5.cloned.1.call-done = bf16[1,768,4096]{2,1,0:T(8,128)(2,1)} async-done(((bf16[1,192,4096]{2,1,0:T(8,128)(2,1)}), bf16[1,768,4096]{2,1,0:T(8,128)(2,1)}) %all-gather.5.cloned.1.call-update) | async-done | bytes 6291472 | tf_op jit(solution)/shard_map/all_gather | solution.py:105
  139.7 31.4 %convolution_convert_fusion.2 = bf16[768,4096]{1,0:T(8,128)(2,1)} fusion(bf16[768,4096]{1,0:T(8,128)(2,1)S(1)} %fusion.19, bf16[4096,4096]{1,0:T(8,128)(2,1)} %param.12), kind=kOutput, calls=%fused_computation.51 | convolution fusion | flops 25772949504 | bytes 46137344 | tf_op jit(solution)/shard_map/td,df->tf/dot_general | solution.py:69
  171.2 71.6 %all-gather.7.cloned.1.call-done = bf16[1,768,4096]{2,1,0:T(8,128)(2,1)} async-done(((bf16[1,192,4096]{2,1,0:T(8,128)(2,1)}), bf16[1,768,4096]{2,1,0:T(8,128)(2,1)}) %all-gather.7.cloned.1.call-update) | async-done | bytes 6291472 | tf_op jit(solution)/shard_map/all_gather | solution.py:106
  242.8 6.7 fusion.138
  249.4 8.8 fusion.26
  258.2 20.9 %multiply_convert_fusion.1 = bf16[768,2048]{1,0:T(8,128)(2,1)} fusion(f32[768,4096]{1,0:T(8,128)} %get-tuple-element.51, bf16[4096,4096]{1,0:T(8,128)(2,1)} %param.13, bf16[1,768,4096]{2,1,0:T(8,128)(2,1)} %all-gather.7.cloned.1.call-done), kind=kOutput, calls=%fused_computation.57 | convolution fusion | flops 12891193344 | bytes 32505856 | tf_op jit(solution)/shard_map/td,fd->tf/dot_general | solution.py:69
  279.1 20.6 %multiply_convert_fusion = bf16[768,2048]{1,0:T(8,128)(2,1)} fusion(f32[768,4096]{1,0:T(8,128)} %get-tuple-element.51, bf16[768,4096]{1,0:T(8,128)(2,1)} %bitcast.293, bf16[4096,4096]{1,0:T(8,128)(2,1)} %param.13), kind=kOutput, calls=%fused_computation.56 | convolution fusion | flops 12891193344 | bytes 32505856 | tf_op jit(solution)/shard_map/td,fd->tf/dot_general | solution.py:69
  299.7 43.6 %convolution_convert_fusion.1 = bf16[768,4096]{1,0:T(8,128)(2,1)} fusion(bf16[4096,4096]{1,0:T(8,128)(2,1)} %param.12, bf16[768,2048]{1,0:T(8,128)(2,1)} %multiply_convert_fusion, bf16[768,2048]{1,0:T(8,128)(2,1)} %multiply_convert_fusion.1), kind=kOutput, calls=%fused_computation.50 | convolution fusion | flops 25785532416 | bytes 46137344 | tf_op jit(solution)/shard_map/tf,df->td/dot_general | solution.py:69
  343.3 4.8 dynamic-slice_bitcast_fusion
  357.6 9.1 convolution_convert_fusion.4
  368.3 15.1 %fusion.31 = f32[768,1536]{0,1:S(1)} fusion(bf16[4096,1536]{0,1:T(8,128)(2,1)} %bitcast.287, bf16[768,4096]{1,0:T(8,128)(2,1)} %bitcast.284, f32[4096]{0:T(1024)S(1)} %bitcast.324, f32[4096]{0:T(1024)S(1)} %bitcast.316, f32[768]{0:T(1024)S(1)} %copy-done.64, f32[768]{0:T(1024)S(1)} %copy-done.62), kind=kOutput, calls=%fused_computation.52 | convolution fusion | flops 9682550784 | bytes 23631872
  390.3 8.7 fusion.13
  399.0 10.4 fusion.117
  409.4 13.1 %fusion.8 = (f32[2,4,768]{2,1,0:T(4,128)S(1)}, bf16[2,4,768,768]{2,3,1,0:T(8,128)(2,1)}) fusion(f32[2,4,768]{2,1,0:T(4,128)S(1)} %multiply_divide_fusion, f32[2,4,768]{2,1,0:T(4,128)S(1)} %get-tuple-element.177, f32[2,768,768,4]{2,1,3,0:T(8,128)} %get-tuple-element.178, pred[768,768]{0,1:T(8,128)(4,1)S(1)} %copy-done.6, ...), kind=kOutput, calls=%fused_computation.15 | convolution fusion | flops 1245702144 | bytes 30941184 | tf_op jit(solution)/shard_map/transpose(jvp(bgqts,bsgh->btgqh))/dot_general | solution.py:53
  422.5 13.5 %fusion.111 = bf16[1,768,2,1,128]{1,4,3,2,0:T(8,128)(2,1)S(1)} fusion(bf16[2,4,768,768]{2,3,1,0:T(8,128)(2,1)} %get-tuple-element.180, f32[2,4,768]{2,1,0:T(4,128)S(1)} %neg.22, f32[2,4,768]{2,1,0:T(4,128)S(1)} %fusion.117, pred[768,768]{0,1:T(8,128)(4,1)S(1)} %copy-done.6, bf16[1,768,2,5,64]{1,4,3,2,0:T(8,128)(2,1)S(1)} %get-tuple-element.128, ...), kind=kOutput, calls=%fused_computation.147 | convolution fusion | flops 1253769216 | bytes 31334400 | tf_op jit(solution)/shard_map/transpose(jvp(btgqh,bsgh->bgqts))/dot_general | solution.py:50
  435.9 13.6 %fusion.93 = bf16[1,768,2,4,128]{1,4,3,2,0:T(8,128)(2,1)S(1)} fusion(bf16[2,4,768,768]{2,3,1,0:T(8,128)(2,1)} %get-tuple-element.180, f32[2,4,768]{2,1,0:T(4,128)S(1)} %neg.22, f32[2,4,768]{2,1,0:T(4,128)S(1)} %fusion.117, pred[768,768]{0,1:T(8,128)(4,1)S(1)} %copy-done.6, bf16[1,768,2,5,64]{1,4,3,2,0:T(8,128)(2,1)S(1)} %get-tuple-element.128, ...), kind=kOutput, calls=%fused_computation.141 | convolution fusion | flops 1251999744 | bytes 32514048 | tf_op jit(solution)/shard_map/transpose(jvp(btgqh,bsgh->bgqts))/dot_general | solution.py:50
  451.9 10.8 fusion.108
  464.3 14.1 %convolution_convert_fusion = bf16[768,4096]{1,0:T(8,128)(2,1)} fusion(bf16[768,1536]{0,1:T(8,128)(2,1)} %bitcast.66, bf16[4096,1536]{0,1:T(8,128)(2,1)S(1)} %bitcast.290), kind=kOutput, calls=%fused_computation.49 | convolution fusion | flops 9666822144 | bytes 21233664 | tf_op jit(solution)/shard_map/tk,dk->td/dot_general | solution.py:69
  478.3 9.9 fusion.86
  497.6 5.4 constant_dynamic-update-slice_fusion.3
  509.3 9.2 collective-permute-done.11
  521.7 18.3 %collective-permute-done.2 = bf16[768,1024]{1,0:T(8,128)(2,1)} collective-permute-done((bf16[768,1024]{1,0:T(8,128)(2,1)}, bf16[768,1024]{1,0:T(8,128)(2,1)}, u32[]{:S(2)}, u32[]{:S(2)}) %collective-permute-start.2) | collective-permute-done | bytes 1572896 | tf_op jit(solution)/shard_map/ppermute | solution.py:57
  552.5 70.7 %collective-permute-done.7 = bf16[768,1024]{1,0:T(8,128)(2,1)S(1)} collective-permute-done((bf16[768,1024]{1,0:T(8,128)(2,1)}, bf16[768,1024]{1,0:T(8,128)(2,1)S(1)}, u32[]{:S(2)}, u32[]{:S(2)}) %collective-permute-start.7) | collective-permute-done | bytes 1572896 | tf_op jit(solution)/shard_map/ppermute | solution.py:57
  626.2 29.6 %collective-permute-done.8 = bf16[768,1024]{1,0:T(8,128)(2,1)S(1)} collective-permute-done((bf16[768,1024]{1,0:T(8,128)(2,1)}, bf16[768,1024]{1,0:T(8,128)(2,1)S(1)}, u32[]{:S(2)}, u32[]{:S(2)}) %collective-permute-start.8) | collective-permute-done | bytes 1572896 | tf_op jit(solution)/shard_map/ppermute | solution.py:57
  662.8 8.6 fusion.137
  671.4 23.1 %collective-permute-done.16 = bf16[768,2048]{1,0:T(8,128)(2,1)} collective-permute-done((bf16[768,2048]{1,0:T(8,128)(2,1)}, bf16[768,2048]{1,0:T(8,128)(2,1)}, u32[]{:S(2)}, u32[]{:S(2)}) %collective-permute-start.16) | collective-permute-done | bytes 3145760 | tf_op jit(solution)/shard_map/ppermute | solution.py:57
  694.7 9.0 add_convert_fusion.2
  703.8 9.4 add_convert_fusion.4
  723.5 4.4 constant_dynamic-update-slice_fusion.4
  727.9 34.1 %collective-permute-done.25 = bf16[768,2048]{1,0:T(8,128)(2,1)} collective-permute-done((bf16[768,2048]{1,0:T(8,128)(2,1)}, bf16[768,2048]{1,0:T(8,128)(2,1)}, u32[]{:S(2)}, u32[]{:S(2)}) %collective-permute-start.25) | collective-permute-done | bytes 3145760 | tf_op jit(solution)/shard_map/ppermute | solution.py:57
  762.6 11.4 %fusion.82 = f32[512,2048]{1,0:T(8,128)} fusion(bf16[3072,512]{1,0:T(8,128)(2,1)S(1)} %copy-done.51, bf16[768,2048]{1,0:T(8,128)(2,1)} %collective-permute-done.17, bf16[768,2048]{1,0:T(8,128)(2,1)} %collective-permute-done.16, bf16[768,2048]{1,0:T(8,128)(2,1)} %collective-permute-done.15, bf16[768,2048]{1,0:T(8,128)(2,1)} %multiply_convert_fusion), kind=kOutput, calls=%fused_computation.118 | convolution fusion | flops 6492782592 | bytes 19922944 | tf_op jit(solution)/shard_map/tr,tc->rc/dot_general | solution.py:69
  773.9 11.3 %fusion.152 = f32[512,2048]{1,0:T(8,128)} fusion(bf16[3072,512]{1,0:T(8,128)(2,1)S(1)} %copy-done.21, bf16[3072,2048]{1,0:T(8,128)(2,1)} %constant_dynamic-update-slice_fusion.4), kind=kOutput, calls=%fused_computation.242 | convolution fusion | flops 6442450944 | bytes 19922944 | tf_op jit(solution)/shard_map/tr,tc->rc/dot_general | solution.py:69
  785.2 27.2 %collective-permute-done.22 = bf16[768,1536]{0,1:T(8,128)(2,1)} collective-permute-done((bf16[768,1536]{0,1:T(8,128)(2,1)}, bf16[768,1536]{0,1:T(8,128)(2,1)}, u32[]{:S(2)}, u32[]{:S(2)}) %collective-permute-start.22) | collective-permute-done | bytes 2359328 | tf_op jit(solution)/shard_map/ppermute | solution.py:57
  812.5 11.5 %fusion.79 = f32[512,2048]{1,0:T(8,128)} fusion(bf16[3072,512]{1,0:T(8,128)(2,1)S(1)} %copy-done.51, bf16[768,2048]{1,0:T(8,128)(2,1)} %collective-permute-done.26, bf16[768,2048]{1,0:T(8,128)(2,1)} %collective-permute-done.25, bf16[768,2048]{1,0:T(8,128)(2,1)} %collective-permute-done.24, bf16[768,2048]{1,0:T(8,128)(2,1)} %multiply_convert_fusion.1), kind=kOutput, calls=%fused_computation.115 | convolution fusion | flops 6492782592 | bytes 19922944 | tf_op jit(solution)/shard_map/tr,tc->rc/dot_general | solution.py:69
  826.1 7.4 fusion.153
  833.5 7.6 fusion.154
  841.7 9.2 fusion.90
  851.0 11.4 %fusion.80 = f32[512,2048]{1,0:T(8,128)} fusion(bf16[3072,512]{1,0:T(8,128)(2,1)S(1)} %copy-done.49, bf16[768,2048]{1,0:T(8,128)(2,1)} %collective-permute-done.26, bf16[768,2048]{1,0:T(8,128)(2,1)} %collective-permute-done.25, bf16[768,2048]{1,0:T(8,128)(2,1)} %collective-permute-done.24, bf16[768,2048]{1,0:T(8,128)(2,1)} %multiply_convert_fusion.1), kind=kOutput, calls=%fused_computation.116 | convolution fusion | flops 6492782592 | bytes 19922944 | tf_op jit(solution)/shard_map/tr,tc->rc/dot_general | solution.py:69
  862.3 11.6 %fusion.81 = f32[512,2048]{1,0:T(8,128)} fusion(bf16[3072,512]{1,0:T(8,128)(2,1)S(1)} %copy-done.49, bf16[768,2048]{1,0:T(8,128)(2,1)} %collective-permute-done.17, bf16[768,2048]{1,0:T(8,128)(2,1)} %collective-permute-done.16, bf16[768,2048]{1,0:T(8,128)(2,1)} %collective-permute-done.15, bf16[768,2048]{1,0:T(8,128)(2,1)} %multiply_convert_fusion), kind=kOutput, calls=%fused_computation.117 | convolution fusion | flops 6492782592 | bytes 19922944 | tf_op jit(solution)/shard_map/tr,tc->rc/dot_general | solution.py:69
  873.9 9.1 fusion.89
  883.0 11.4 %fusion.156 = f32[512,2048]{1,0:T(8,128)} fusion(bf16[3072,512]{1,0:T(8,128)(2,1)S(1)} %pad_maximum_fusion.7, bf16[3072,2048]{1,0:T(8,128)(2,1)} %constant_dynamic-update-slice_fusion.4), kind=kOutput, calls=%fused_computation.246 | convolution fusion | flops 6442450944 | bytes 19922944 | tf_op jit(solution)/shard_map/tr,tc->rc/dot_general | solution.py:69
  894.5 7.5 fusion.158
  902.0 8.5 fusion.155
  913.5 4.8 fusion.73
  935.0 106.3 %collective-permute-done.33 = f32[128,2048]{1,0:T(8,128)S(1)} collective-permute-done((f32[128,2048]{1,0:T(8,128)S(1)}, f32[128,2048]{1,0:T(8,128)S(1)}, u32[]{:S(2)}, u32[]{:S(2)}) %collective-permute-start.33) | collective-permute-done | bytes 1048608 | tf_op jit(solution)/shard_map/ppermute | solution.py:57
  1068.8 6.5 pad_maximum_fusion.4
  1075.3 37.2 %collective-permute-done.32 = f32[512,1536]{1,0:T(8,128)} collective-permute-done((f32[512,1536]{1,0:T(8,128)}, f32[512,1536]{1,0:T(8,128)}, u32[]{:S(2)}, u32[]{:S(2)}) %collective-permute-start.32) | collective-permute-done | bytes 3145760 | tf_op jit(solution)/shard_map/ppermute | solution.py:57
  (361 shorter events, 154.1 us)
Async XLA Ops:
  7.2 120.5 %all-gather.5.cloned.1.call-start = ((), (), s32[]{:S(2)}) async-start(), calls=%async_computation.4 | async-start | bytes 7864320 | tf_op jit(solution)/shard_map/all_gather | solution.py:105
  7.9 234.8 %all-gather.7.cloned.1.call-start = ((), (), s32[]{:S(2)}) async-start(), calls=%async_computation.5 | async-start | bytes 7864320 | tf_op jit(solution)/shard_map/all_gather | solution.py:106
  8.7 904.8 %reduce-scatter.5.cloned.1.call-start = ((), (), s32[]{:S(2)}) async-start(), calls=%async_computation.3 | async-start | bytes 7864320 | tf_op jit(solution)/shard_map/reduce_scatter | solution.py:166
  134.7 359.3 %collective-permute-start.5 = (f32[768,2]{0,1:T(2,128)}, f32[768,2]{0,1:T(2,128)}, u32[]{:S(2)}, u32[]{:S(2)}) collective-permute-start(f32[768,2]{0,1:T(2,128)} %pad_maximum_fusion.31), channel_id=1, source_target_pairs={{0,3},{1,2},{2,1},{3,0},{4,7},{5,6},{6,5},{7,4},{8,11},{9,10},{10,... | collective-permute-start | bytes 18440 | tf_op jit(solution)/shard_map/ppermute | solution.py:57
  135.7 358.3 %collective-permute-start.4 = (f32[768,2]{0,1:T(2,128)}, f32[768,2]{0,1:T(2,128)}, u32[]{:S(2)}, u32[]{:S(2)}) collective-permute-start(f32[768,2]{0,1:T(2,128)} %pad_maximum_fusion.31), channel_id=1, source_target_pairs={{0,2},{1,3},{2,0},{3,1},{4,6},{5,7},{6,4},{7,5},{8,10},{9,11},{10,... | collective-permute-start | bytes 18440 | tf_op jit(solution)/shard_map/ppermute | solution.py:57
  349.6 169.0 %collective-permute-start = (bf16[768,1024]{1,0:T(8,128)(2,1)}, bf16[768,1024]{1,0:T(8,128)(2,1)}, u32[]{:S(2)}, u32[]{:S(2)}) collective-permute-start(bf16[768,1024]{1,0:T(8,128)(2,1)} %pad_maximum_fusion.17), channel_id=1, source_target_pairs={{0,1},{1,0},{2,3},{3,2},{4,5},{5,4},{6,7},{7,6},{8,9},{9,8},{10,11... | collective-permute-start | bytes 4718600 | tf_op jit(solution)/shard_map/ppermute | solution.py:57
  350.9 168.5 %collective-permute-start.1 = (bf16[768,1024]{1,0:T(8,128)(2,1)}, bf16[768,1024]{1,0:T(8,128)(2,1)}, u32[]{:S(2)}, u32[]{:S(2)}) collective-permute-start(bf16[768,1024]{1,0:T(8,128)(2,1)} %pad_maximum_fusion.18), channel_id=1, source_target_pairs={{0,2},{1,3},{2,0},{3,1},{4,6},{5,7},{6,4},{7,5},{8,10},{9,11},{10,... | collective-permute-start | bytes 4718600 | tf_op jit(solution)/shard_map/ppermute | solution.py:57
  352.4 188.2 %collective-permute-start.13 = (bf16[768,2048]{1,0:T(8,128)(2,1)}, bf16[768,2048]{1,0:T(8,128)(2,1)}, u32[]{:S(2)}, u32[]{:S(2)}) collective-permute-start(bf16[768,2048]{1,0:T(8,128)(2,1)} %get-tuple-element.49), channel_id=1, source_target_pairs={{0,4},{1,5},{2,6},{3,7},{4,0},{5,1},{6,2},{7,3},{8,12},{9,13},{10,... | collective-permute-start | bytes 9437192 | tf_op jit(solution)/shard_map/ppermute | solution.py:57
  387.5 526.0 %reduce-scatter.3.cloned.1.call-start = ((), (), s32[]{:S(2)}) async-start(), calls=%async_computation.2 | async-start | bytes 7864320 | tf_op jit(solution)/shard_map/reduce_scatter | solution.py:154
  494.0 1.4 collective-permute-start.3
  494.1 9.0 collective-permute-start.9
  495.4 11.3 collective-permute-start.10
  503.1 36.9 %collective-permute-start.2 = (bf16[768,1024]{1,0:T(8,128)(2,1)}, bf16[768,1024]{1,0:T(8,128)(2,1)}, u32[]{:S(2)}, u32[]{:S(2)}) collective-permute-start(bf16[768,1024]{1,0:T(8,128)(2,1)} %pad_maximum_fusion.19), channel_id=1, source_target_pairs={{0,3},{1,2},{2,1},{3,0},{4,7},{5,6},{6,5},{7,4},{8,11},{9,10},{10,... | collective-permute-start | bytes 4718600 | tf_op jit(solution)/shard_map/ppermute | solution.py:57
  506.7 11.7 %collective-permute-start.11 = (bf16[768,256]{0,1:T(8,128)(2,1)}, bf16[768,256]{0,1:T(8,128)(2,1)}, u32[]{:S(2)}, u32[]{:S(2)}) collective-permute-start(bf16[768,256]{0,1:T(8,128)(2,1)} %pad_maximum_fusion.28), channel_id=1, source_target_pairs={{0,5},{1,4},{2,7},{3,6},{4,1},{5,0},{6,3},{7,2},{8,13},{9,12},{10,... | collective-permute-start | bytes 1179656 | tf_op jit(solution)/shard_map/ppermute | solution.py:57
  518.4 139.4 %collective-permute-start.12 = (bf16[768,2048]{1,0:T(8,128)(2,1)}, bf16[768,2048]{1,0:T(8,128)(2,1)S(1)}, u32[]{:S(2)}, u32[]{:S(2)}) collective-permute-start(bf16[768,2048]{1,0:T(8,128)(2,1)} %get-tuple-element.49), channel_id=1, source_target_pairs={{0,1},{1,0},{2,3},{3,2},{4,5},{5,4},{6,7},{7,6},{8,9},{9,8},{10,11... | collective-permute-start | bytes 9437192 | tf_op jit(solution)/shard_map/ppermute | solution.py:57
  518.5 139.3 %collective-permute-start.19 = (bf16[768,2048]{1,0:T(8,128)(2,1)S(1)}, bf16[768,2048]{1,0:T(8,128)(2,1)S(1)}, u32[]{:S(2)}, u32[]{:S(2)}) collective-permute-start(bf16[768,2048]{1,0:T(8,128)(2,1)S(1)} %copy-done.5), channel_id=1, source_target_pairs={{0,4},{1,5},{2,6},{3,7},{4,0},{5,1},{6,2},{7,3},{8,12},{9,13},{10,... | collective-permute-start | bytes 9437192 | tf_op jit(solution)/shard_map/ppermute | solution.py:57
  519.4 22.5 %collective-permute-start.6 = (bf16[768,1024]{1,0:T(8,128)(2,1)}, bf16[768,1024]{1,0:T(8,128)(2,1)S(1)}, u32[]{:S(2)}, u32[]{:S(2)}) collective-permute-start(bf16[768,1024]{1,0:T(8,128)(2,1)} %pad_maximum_fusion.21), channel_id=1, source_target_pairs={{0,1},{1,0},{2,3},{3,2},{4,5},{5,4},{6,7},{7,6},{8,9},{9,8},{10,11... | collective-permute-start | bytes 4718600 | tf_op jit(solution)/shard_map/ppermute | solution.py:57
  540.0 83.2 %collective-permute-start.7 = (bf16[768,1024]{1,0:T(8,128)(2,1)}, bf16[768,1024]{1,0:T(8,128)(2,1)S(1)}, u32[]{:S(2)}, u32[]{:S(2)}) collective-permute-start(bf16[768,1024]{1,0:T(8,128)(2,1)} %pad_maximum_fusion.22), channel_id=1, source_target_pairs={{0,4},{1,5},{2,6},{3,7},{4,0},{5,1},{6,2},{7,3},{8,12},{9,13},{10,... | collective-permute-start | bytes 4718600 | tf_op jit(solution)/shard_map/ppermute | solution.py:57
  540.6 120.6 %collective-permute-start.14 = (bf16[768,2048]{1,0:T(8,128)(2,1)}, bf16[768,2048]{1,0:T(8,128)(2,1)S(1)}, u32[]{:S(2)}, u32[]{:S(2)}) collective-permute-start(bf16[768,2048]{1,0:T(8,128)(2,1)} %collective-permute-done.13), channel_id=1, source_target_pairs={{0,1},{1,0},{2,3},{3,2},{4,5},{5,4},{6,7},{7,6},{8,9},{9,8},{10,11... | collective-permute-start | bytes 9437192 | tf_op jit(solution)/shard_map/ppermute | solution.py:57
  540.6 118.0 %slice-start = ((s8[12582912]{0:T(1024)(128)(4,1)}), s8[4194304]{0:T(1024)(128)(4,1)S(1)}, s32[]{:S(2)}) async-start(s8[12582912]{0:T(1024)(128)(4,1)} %bitcast.280), calls=%async_computation.6 | async-start | bytes 8388608
  541.9 113.9 %collective-permute-start.8 = (bf16[768,1024]{1,0:T(8,128)(2,1)}, bf16[768,1024]{1,0:T(8,128)(2,1)S(1)}, u32[]{:S(2)}, u32[]{:S(2)}) collective-permute-start(bf16[768,1024]{1,0:T(8,128)(2,1)} %pad_maximum_fusion.23), channel_id=1, source_target_pairs={{0,5},{1,4},{2,7},{3,6},{4,1},{5,0},{6,3},{7,2},{8,13},{9,12},{10,... | collective-permute-start | bytes 4718600 | tf_op jit(solution)/shard_map/ppermute | solution.py:57
  547.1 111.5 %slice-start.1 = ((s8[12582912]{0:T(1024)(128)(4,1)}), s8[4194304]{0:T(1024)(128)(4,1)S(1)}, s32[]{:S(2)}) async-start(s8[12582912]{0:T(1024)(128)(4,1)} %bitcast.280), calls=%async_computation.7 | async-start | bytes 8388608
  623.2 71.3 %collective-permute-start.16 = (bf16[768,2048]{1,0:T(8,128)(2,1)}, bf16[768,2048]{1,0:T(8,128)(2,1)}, u32[]{:S(2)}, u32[]{:S(2)}) collective-permute-start(bf16[768,2048]{1,0:T(8,128)(2,1)} %multiply_convert_fusion), channel_id=1, source_target_pairs={{0,2},{1,3},{2,0},{3,1},{4,6},{5,7},{6,4},{7,5},{8,10},{9,11},{10,... | collective-permute-start | bytes 9437192 | tf_op jit(solution)/shard_map/ppermute | solution.py:57
  655.8 60.6 %collective-permute-start.18 = (bf16[768,2048]{1,0:T(8,128)(2,1)S(1)}, bf16[768,2048]{1,0:T(8,128)(2,1)}, u32[]{:S(2)}, u32[]{:S(2)}) collective-permute-start(bf16[768,2048]{1,0:T(8,128)(2,1)S(1)} %copy-done.5), channel_id=1, source_target_pairs={{0,1},{1,0},{2,3},{3,2},{4,5},{5,4},{6,7},{7,6},{8,9},{9,8},{10,11... | collective-permute-start | bytes 9437192 | tf_op jit(solution)/shard_map/ppermute | solution.py:57
  657.8 70.0 %collective-permute-start.15 = (bf16[768,2048]{1,0:T(8,128)(2,1)}, bf16[768,2048]{1,0:T(8,128)(2,1)}, u32[]{:S(2)}, u32[]{:S(2)}) collective-permute-start(bf16[768,2048]{1,0:T(8,128)(2,1)} %multiply_convert_fusion), channel_id=1, source_target_pairs={{0,1},{1,0},{2,3},{3,2},{4,5},{5,4},{6,7},{7,6},{8,9},{9,8},{10,11... | collective-permute-start | bytes 9437192 | tf_op jit(solution)/shard_map/ppermute | solution.py:57
  657.8 104.1 %collective-permute-start.25 = (bf16[768,2048]{1,0:T(8,128)(2,1)}, bf16[768,2048]{1,0:T(8,128)(2,1)}, u32[]{:S(2)}, u32[]{:S(2)}) collective-permute-start(bf16[768,2048]{1,0:T(8,128)(2,1)} %multiply_convert_fusion.1), channel_id=1, source_target_pairs={{0,2},{1,3},{2,0},{3,1},{4,6},{5,7},{6,4},{7,5},{8,10},{9,11},{10,... | collective-permute-start | bytes 9437192 | tf_op jit(solution)/shard_map/ppermute | solution.py:57
  661.2 61.7 %collective-permute-start.20 = (bf16[768,2048]{1,0:T(8,128)(2,1)S(1)}, bf16[768,2048]{1,0:T(8,128)(2,1)}, u32[]{:S(2)}, u32[]{:S(2)}) collective-permute-start(bf16[768,2048]{1,0:T(8,128)(2,1)S(1)} %collective-permute-done.19), channel_id=1, source_target_pairs={{0,1},{1,0},{2,3},{3,2},{4,5},{5,4},{6,7},{7,6},{8,9},{9,8},{10,11... | collective-permute-start | bytes 9437192 | tf_op jit(solution)/shard_map/ppermute | solution.py:57
  694.5 67.4 %collective-permute-start.17 = (bf16[768,2048]{1,0:T(8,128)(2,1)}, bf16[768,2048]{1,0:T(8,128)(2,1)}, u32[]{:S(2)}, u32[]{:S(2)}) collective-permute-start(bf16[768,2048]{1,0:T(8,128)(2,1)} %collective-permute-done.16), channel_id=1, source_target_pairs={{0,1},{1,0},{2,3},{3,2},{4,5},{5,4},{6,7},{7,6},{8,9},{9,8},{10,11... | collective-permute-start | bytes 9437192 | tf_op jit(solution)/shard_map/ppermute | solution.py:57
  716.4 96.1 %collective-permute-start.24 = (bf16[768,2048]{1,0:T(8,128)(2,1)}, bf16[768,2048]{1,0:T(8,128)(2,1)}, u32[]{:S(2)}, u32[]{:S(2)}) collective-permute-start(bf16[768,2048]{1,0:T(8,128)(2,1)} %multiply_convert_fusion.1), channel_id=1, source_target_pairs={{0,1},{1,0},{2,3},{3,2},{4,5},{5,4},{6,7},{7,6},{8,9},{9,8},{10,11... | collective-permute-start | bytes 9437192 | tf_op jit(solution)/shard_map/ppermute | solution.py:57
  722.9 89.6 %collective-permute-start.22 = (bf16[768,1536]{0,1:T(8,128)(2,1)}, bf16[768,1536]{0,1:T(8,128)(2,1)}, u32[]{:S(2)}, u32[]{:S(2)}) collective-permute-start(bf16[768,1536]{0,1:T(8,128)(2,1)} %bitcast.66), channel_id=1, source_target_pairs={{0,2},{1,3},{2,0},{3,1},{4,6},{5,7},{6,4},{7,5},{8,10},{9,11},{10,... | collective-permute-start | bytes 7077896 | tf_op jit(solution)/shard_map/ppermute | solution.py:57
  727.9 113.2 %collective-permute-start.21 = (bf16[768,1536]{0,1:T(8,128)(2,1)}, bf16[768,1536]{0,1:T(8,128)(2,1)}, u32[]{:S(2)}, u32[]{:S(2)}) collective-permute-start(bf16[768,1536]{0,1:T(8,128)(2,1)} %bitcast.66), channel_id=1, source_target_pairs={{0,1},{1,0},{2,3},{3,2},{4,5},{5,4},{6,7},{7,6},{8,9},{9,8},{10,11... | collective-permute-start | bytes 7077896 | tf_op jit(solution)/shard_map/ppermute | solution.py:57
  761.9 50.6 %collective-permute-start.26 = (bf16[768,2048]{1,0:T(8,128)(2,1)}, bf16[768,2048]{1,0:T(8,128)(2,1)}, u32[]{:S(2)}, u32[]{:S(2)}) collective-permute-start(bf16[768,2048]{1,0:T(8,128)(2,1)} %collective-permute-done.25), channel_id=1, source_target_pairs={{0,1},{1,0},{2,3},{3,2},{4,5},{5,4},{6,7},{7,6},{8,9},{9,8},{10,11... | collective-permute-start | bytes 9437192 | tf_op jit(solution)/shard_map/ppermute | solution.py:57
  761.9 286.8 %collective-permute-start.37 = (f32[512,2048]{1,0:T(8,128)}, f32[512,2048]{1,0:T(8,128)}, u32[]{:S(2)}, u32[]{:S(2)}) collective-permute-start(f32[512,2048]{1,0:T(8,128)} %fusion.137), channel_id=1, source_target_pairs={{0,2},{1,3},{2,0},{3,1},{4,6},{5,7},{6,4},{7,5},{8,10},{9,11},{10,... | collective-permute-start | bytes 12582920 | tf_op jit(solution)/shard_map/ppermute | solution.py:57
  812.5 29.3 %collective-permute-start.23 = (bf16[768,1536]{0,1:T(8,128)(2,1)}, bf16[768,1536]{0,1:T(8,128)(2,1)}, u32[]{:S(2)}, u32[]{:S(2)}) collective-permute-start(bf16[768,1536]{0,1:T(8,128)(2,1)} %collective-permute-done.22), channel_id=1, source_target_pairs={{0,1},{1,0},{2,3},{3,2},{4,5},{5,4},{6,7},{7,6},{8,9},{9,8},{10,11... | collective-permute-start | bytes 7077896 | tf_op jit(solution)/shard_map/ppermute | solution.py:57
  824.0 230.5 %collective-permute-start.35 = (f32[512,2048]{1,0:T(8,128)}, f32[512,2048]{1,0:T(8,128)}, u32[]{:S(2)}, u32[]{:S(2)}) collective-permute-start(f32[512,2048]{1,0:T(8,128)} %fusion.79), channel_id=1, source_target_pairs={{0,4},{1,5},{2,6},{3,7},{4,0},{5,1},{6,2},{7,3},{8,12},{9,13},{10,... | collective-permute-start | bytes 12582920 | tf_op jit(solution)/shard_map/ppermute | solution.py:57
  824.9 233.7 %collective-permute-start.36 = (f32[512,2048]{1,0:T(8,128)}, f32[512,2048]{1,0:T(8,128)}, u32[]{:S(2)}, u32[]{:S(2)}) collective-permute-start(f32[512,2048]{1,0:T(8,128)} %fusion.82), channel_id=1, source_target_pairs={{0,4},{1,5},{2,6},{3,7},{4,0},{5,1},{6,2},{7,3},{8,12},{9,13},{10,... | collective-permute-start | bytes 12582920 | tf_op jit(solution)/shard_map/ppermute | solution.py:57
  841.1 88.3 %collective-permute-start.34 = (f32[128,2048]{1,0:T(8,128)}, f32[128,2048]{1,0:T(8,128)}, u32[]{:S(2)}, u32[]{:S(2)}) collective-permute-start(f32[128,2048]{1,0:T(8,128)} %fusion.154), channel_id=1, source_target_pairs={{0,2},{1,3},{2,0},{3,1},{4,6},{5,7},{6,4},{7,5},{8,10},{9,11},{10,... | collective-permute-start | bytes 3145736 | tf_op jit(solution)/shard_map/ppermute | solution.py:57
  918.4 4.3 collective-permute-start.27
  922.8 5.4 collective-permute-start.28
  923.9 123.3 %copy-start.17 = (f32[128,2048]{1,0:T(8,128)S(1)}, f32[128,2048]{1,0:T(8,128)}, u32[]{:S(2)}) copy-start(f32[128,2048]{1,0:T(8,128)} %fusion.158) | copy-start | bytes 3145732
  928.2 133.5 %collective-permute-start.38 = (f32[512,2048]{1,0:T(8,128)}, f32[512,2048]{1,0:T(8,128)S(1)}, u32[]{:S(2)}, u32[]{:S(2)}) collective-permute-start(f32[512,2048]{1,0:T(8,128)} %fusion.152), channel_id=1, source_target_pairs={{0,2},{1,3},{2,0},{3,1},{4,6},{5,7},{6,4},{7,5},{8,10},{9,11},{10,... | collective-permute-start | bytes 12582920 | tf_op jit(solution)/shard_map/ppermute | solution.py:57
  929.4 1.3 collective-permute-start.29
  929.5 119.0 %copy-start.18 = (f32[128,2048]{1,0:T(8,128)S(1)}, f32[128,2048]{1,0:T(8,128)}, u32[]{:S(2)}) copy-start(f32[128,2048]{1,0:T(8,128)} %fusion.157) | copy-start | bytes 3145732
  930.7 110.6 %collective-permute-start.33 = (f32[128,2048]{1,0:T(8,128)S(1)}, f32[128,2048]{1,0:T(8,128)S(1)}, u32[]{:S(2)}, u32[]{:S(2)}) collective-permute-start(f32[128,2048]{1,0:T(8,128)S(1)} %copy-done.55), channel_id=1, source_target_pairs={{0,2},{1,3},{2,0},{3,1},{4,6},{5,7},{6,4},{7,5},{8,10},{9,11},{10,... | collective-permute-start | bytes 3145736 | tf_op jit(solution)/shard_map/ppermute | solution.py:57
  935.0 116.4 %copy-start.16 = (f32[512,2048]{1,0:T(8,128)S(1)}, f32[512,2048]{1,0:T(8,128)}, u32[]{:S(2)}) copy-start(f32[512,2048]{1,0:T(8,128)} %fusion.155) | copy-start | bytes 12582916
  1041.3 5.0 collective-permute-start.30
  1046.3 66.2 %collective-permute-start.32 = (f32[512,1536]{1,0:T(8,128)}, f32[512,1536]{1,0:T(8,128)}, u32[]{:S(2)}, u32[]{:S(2)}) collective-permute-start(f32[512,1536]{1,0:T(8,128)} %fusion.90), channel_id=1, source_target_pairs={{0,4},{1,5},{2,6},{3,7},{4,0},{5,1},{6,2},{7,3},{8,12},{9,13},{10,... | collective-permute-start | bytes 9437192 | tf_op jit(solution)/shard_map/ppermute | solution.py:57
  1048.7 9.2 collective-permute-start.31
  (91 other events, 1230.5 us)
Sparse Core Ops, SparseCore 0:
  9.6 118.0 all-gather.4
  129.2 113.5 all-gather.6
  387.6 107.9 reduce-scatter.4
  508.6 108.6 reduce-scatter.2

commit v2 on v1

--- a/solution.py
+++ b/solution.py
@@ -146,23 +146,26 @@
             far_hidden.append(swap(d_hid, XAX))
             tied, _ = hold(dy_full, d_hid)
 
+        tied, hm_send = hold(dy_full, hm_send)
         d_ctx = mm('td,cd->tc', tied, w_out).astype(BF16)
         (d_proj,) = attn_pull(d_ctx.reshape(context.shape))
         d_flat, = hold(d_proj.reshape(seq_len, -1))
         far_proj = swap(d_flat, XAX)
         d_hattn_part, = hold(mm('tk,dk->td', d_flat, w_qkv.reshape(d_model, -1)).astype(BF16))
+        gelu_keep, gelu_send = halves(gelu_parts)
+        gelu_send, d_hattn_part = hold(gelu_send, d_hattn_part)
         d_hattn = lax.psum_scatter(d_hattn_part, 'tp', scatter_dimension=0, tiled=True)
-        gelu_keep, gelu_send = halves(gelu_parts)
         ctx_keep, ctx_send = halves(ctx_parts)
 
         grad = lambda lhs4, rhs4: hold(mm('tr,tc->rc', lhs4, rhs4))[0]
         after = lambda value, *earlier: hold(value, *earlier)[0]
         up4_0 = stack4(d_hidden[0], far_hidden[0])
-        up0 = grad(after(hm_send, d_hattn_part), up4_0)
+        up0 = grad(hm_send, up4_0)
         came_up0 = swap(up0, YAX)
         dy4_0 = stack4(dy_lo, far_lo)
         hid_cat = jnp.concatenate(d_hidden, axis=1)
         d_hmlp_part, = hold(mm('tf,df->td', hid_cat, w_up).astype(BF16))
+        hm_send, d_hmlp_part = hold(hm_send, d_hmlp_part)
         d_hmlp = lax.psum_scatter(d_hmlp_part, 'tp', scatter_dimension=0, tiled=True)
         down0 = grad(gelu_send, dy4_0)
         came_down0 = swap(down0, XAX)
@@ -197,13 +200,13 @@
         grad_ln = grad_ln + swap(grad_ln, CORE)
         (kept_up[0], kept_up[1], kept_down[0], kept_down[1], kept_out[0], kept_out[1], kept_qkv, grad_x, grad_ln) = hold(
             *kept_up, *kept_down, *kept_out, kept_qkv, grad_x, grad_ln)
-        for bit in (YAX, XAX):
-            grad_ln = grad_ln + swap(grad_ln, bit)
+        grad_ln = (grad_ln + swap(grad_ln, XAX)) + (swap(grad_ln, YAX) + swap(grad_ln, YAX | XAX))
 
         join = lambda kept, came: jnp.concatenate([k + c for k, c in zip(kept, came)], axis=1)
         grad_wqkv = (kept_qkv + came_qkv).reshape((-1,) + w_qkv.shape[1:])
         grad_wup = join(kept_up, (came_up0, came_up1))
         grad_wdown = join(kept_down, (came_down0, came_down1))
+        kept_out[0], kept_out[1], grad_wqkv, grad_wup, grad_wdown = hold(*kept_out, grad_wqkv, grad_wup, grad_wdown)
         return grad_x, grad_ln, grad_wqkv, join(kept_out, came_out), grad_wup, grad_wdown
 
     act_spec = P('dp', 'tp', None)

time: 1140 us -> 954 us (0.84)
  waiting for transfers between devices: 526 us -> 353 us
  matrix products: 354 us -> 339 us
    ppermute x37 -> x38, waiting for transfers between devices: 365 us -> 246 us  [swap(): return lax.ppermute(value, 'dp', [(i, i ^ bit) for i in range(8)])]
    all_gather x1, waiting for transfers between devices: 71.6 us -> 12.5 us  [local_body(): dy_all = lax.all_gather(dy_loc, 'tp', axis=0, tiled=True)]
    ppermute x37 -> x38, starting transfers between devices: 22.6 us -> 28.1 us  [swap(): return lax.ppermute(value, 'dp', [(i, i ^ bit) for i in range(8)])]
    unnamed x199 -> x145, local copies, waits for them, and re-layouts: 55.6 us -> 60.1 us
  transfers between devices with their start and end apart: 43 -> 44, of which waited for: 17 -> 13; matrix products, arithmetic and copies ran while one was open for 48% -> 57% of each run, Pallas kernels for 0% -> 0%
where the time goes in v2:
time: 954 us; the launch traced here: 943 us
  waiting for transfers between devices  353 us (37%)
  matrix products  339 us (36%)
  other arithmetic  114 us (12%)
  local copies, waits for them, and re-layouts  92.3 us (10%)
  starting transfers between devices  28.8 us (3%)
  between operations  15.3 us (2%)
    dot_general x20, matrix products, mm(): return jnp.einsum(spec, lhs, rhs, preferred_element_type=F32)  260 us
    ppermute x38, waiting for transfers between devices, swap(): return lax.ppermute(value, 'dp', [(i, i ^ bit) for i in range(8)])  246 us
    all_gather x1, waiting for transfers between devices, local_body(): x_full = lax.all_gather(x_loc, 'tp', axis=0, tiled=True)  84.7 us
    unnamed x145, local copies, waits for them, and re-layouts  60.1 us
    dot_general x3, matrix products, attention_core(): jnp.einsum('btgqh,bsgh->bgqts', query_rot, key_rot, preferred_element_typ...  35.6 us
    dot_general x3, matrix products, attention_core(): jnp.einsum('bgqts,bsgh->btgqh', attn_probs, values, preferred_element_typ...  31.7 us
    ppermute x38, starting transfers between devices, swap(): return lax.ppermute(value, 'dp', [(i, i ^ bit) for i in range(8)])  28.1 us
    convert_element_type x3, other arithmetic, norm_apply(): ((x_rows.astype(F32) - row_mean) * row_rstd * norm_gain + norm_shift).ast...  21.4 us
  transfers between devices with their start and end apart: 44, of which 13 were waited for; matrix products, arithmetic and copies ran while one was open for 57% of the time, Pallas kernels for 0%

profile of v2, /device:TPU:0, one launch (start us, length us, event | category | flops | bytes accessed | tf_op | source)
XLA Modules:
  0.0 942.7 jit_solution(2505519016709030233)
XLA Ops:
  9.5 31.3 %copy.21 = bf16[4096,2,6,128]{0,3,2,1:T(8,128)(2,1)} copy(bf16[4096,2,6,128]{3,1,2,0:T(2,128)(2,1)} %param.10) | data formatting | bytes 25165824 | tf_op args[3]
  42.9 84.7 %all-gather.5.cloned.1.call-done = bf16[1,768,4096]{2,1,0:T(8,128)(2,1)} async-done(((bf16[1,192,4096]{2,1,0:T(8,128)(2,1)}), bf16[1,768,4096]{2,1,0:T(8,128)(2,1)}) %all-gather.5.cloned.1.call-update) | async-done | bytes 6291472 | tf_op jit(solution)/shard_map/all_gather | solution.py:105
  146.7 31.4 %convolution_convert_fusion.2 = bf16[768,4096]{1,0:T(8,128)(2,1)} fusion(bf16[768,4096]{1,0:T(8,128)(2,1)S(1)} %fusion.19, bf16[4096,4096]{1,0:T(8,128)(2,1)} %param.12), kind=kOutput, calls=%fused_computation.51 | convolution fusion | flops 25772949504 | bytes 46137344 | tf_op jit(solution)/shard_map/td,df->tf/dot_general | solution.py:69
  178.1 12.7 %fusion.26 = (f32[768,4096]{1,0:T(8,128)}, bf16[768,4096]{1,0:T(8,128)(2,1)S(1)}) fusion(bf16[768,4096]{1,0:T(8,128)(2,1)} %convolution_convert_fusion.2), kind=kLoop, calls=%fused_computation.38 | loop fusion | flops 34603008 | bytes 25165824 | tf_op jit(solution)/shard_map/add | solution.py:121
  195.3 12.3 %fusion.31 = f32[768,1536]{0,1} fusion(bf16[4096,1536]{0,1:T(8,128)(2,1)S(1)} %bitcast.288, bf16[768,4096]{1,0:T(8,128)(2,1)S(1)} %bitcast.285, f32[4096]{0:T(1024)S(1)} %bitcast.325, f32[4096]{0:T(1024)S(1)} %bitcast.317, f32[768]{0:T(1024)S(1)} %add_rsqrt_fusion, f32[768]{0:T(1024)S(1)} %broadcast_multiply_fusion), kind=kOutput, calls=%fused_computation.52 | convolution fusion | flops 9682550784 | bytes 23631872
  211.6 8.4 fusion.13
  220.0 10.2 %fusion.117 = f32[2,4,768]{2,1,0:T(4,128)S(1)} fusion(f32[2,4,768]{2,1,0:T(4,128)S(1)} %get-tuple-element.195, f32[2,768,768,4]{2,1,3,0:T(8,128)} %get-tuple-element.196, pred[768,768]{0,1:T(8,128)(4,1)S(1)} %iota_compare_fusion), kind=kLoop, calls=%fused_computation.164 | loop fusion | flops 18868224 | bytes 19513344 | tf_op jit(solution)/shard_map/jvp()/reduce_sum | solution.py:52
  230.3 12.5 %all-gather.7.cloned.1.call-done = bf16[1,768,4096]{2,1,0:T(8,128)(2,1)} async-done(((bf16[1,192,4096]{2,1,0:T(8,128)(2,1)}), bf16[1,768,4096]{2,1,0:T(8,128)(2,1)}) %all-gather.7.cloned.1.call-update) | async-done | bytes 6291472 | tf_op jit(solution)/shard_map/all_gather | solution.py:106
  242.8 20.6 %multiply_convert_fusion.1 = bf16[768,2048]{1,0:T(8,128)(2,1)} fusion(f32[768,4096]{1,0:T(8,128)} %get-tuple-element.61, bf16[4096,4096]{1,0:T(8,128)(2,1)} %param.13, bf16[1,768,4096]{2,1,0:T(8,128)(2,1)} %all-gather.7.cloned.1.call-done), kind=kOutput, calls=%fused_computation.57 | convolution fusion | flops 12891193344 | bytes 32505856 | tf_op jit(solution)/shard_map/td,fd->tf/dot_general | solution.py:69
  263.4 6.6 fusion.137
  270.0 21.0 %multiply_convert_fusion = bf16[768,2048]{1,0:T(8,128)(2,1)} fusion(f32[768,4096]{1,0:T(8,128)} %get-tuple-element.61, bf16[768,4096]{1,0:T(8,128)(2,1)} %bitcast.294, bf16[4096,4096]{1,0:T(8,128)(2,1)} %param.13), kind=kOutput, calls=%fused_computation.56 | convolution fusion | flops 12891193344 | bytes 32505856 | tf_op jit(solution)/shard_map/td,fd->tf/dot_general | solution.py:69
  308.2 9.0 add_convert_fusion.4
  317.2 9.0 add_convert_fusion.2
  326.2 10.2 %convolution_convert_fusion.4 = bf16[768,1024]{1,0:T(8,128)(2,1)} fusion(bf16[768,4096]{1,0:T(8,128)(2,1)S(1)} %bitcast.297, bf16[1024,4096]{1,0:T(8,128)(2,1)} %param.11), kind=kOutput, calls=%fused_computation.128 | convolution fusion | flops 6443237376 | bytes 16252928 | tf_op jit(solution)/shard_map/td,cd->tc/dot_general | solution.py:69
  339.0 12.6 %fusion.8 = (f32[2,4,768]{2,1,0:T(4,128)S(1)}, bf16[2,4,768,768]{2,3,1,0:T(8,128)(2,1)}) fusion(f32[2,4,768]{2,1,0:T(4,128)S(1)} %multiply_divide_fusion, f32[2,4,768]{2,1,0:T(4,128)S(1)} %get-tuple-element.195, f32[2,768,768,4]{2,1,3,0:T(8,128)} %get-tuple-element.196, pred[768,768]{0,1:T(8,128)(4,1)S(1)} %iota_compare_fusion, ...), kind=kOutput, calls=%fused_computation.15 | convolution fusion | flops 1245702144 | bytes 30941184 | tf_op jit(solution)/shard_map/transpose(jvp(bgqts,bsgh->btgqh))/dot_general | solution.py:53
  351.6 13.4 %fusion.93 = bf16[1,768,2,4,128]{1,4,3,2,0:T(8,128)(2,1)S(1)} fusion(bf16[2,4,768,768]{2,3,1,0:T(8,128)(2,1)} %get-tuple-element.198, f32[2,4,768]{2,1,0:T(4,128)S(1)} %neg.22, f32[2,4,768]{2,1,0:T(4,128)S(1)} %fusion.117, pred[768,768]{0,1:T(8,128)(4,1)S(1)} %iota_compare_fusion, bf16[1,768,2,5,64]{1,4,3,2,0:T(8,128)(2,1)S(1)} %get-tuple-element.146, ...), kind=kOutput, calls=%fused_computation.141 | convolution fusion | flops 1251999744 | bytes 32514048 | tf_op jit(solution)/shard_map/transpose(jvp(btgqh,bsgh->bgqts))/dot_general | solution.py:50
  365.0 13.8 %fusion.111 = bf16[1,768,2,1,128]{1,4,3,2,0:T(8,128)(2,1)S(1)} fusion(bf16[2,4,768,768]{2,3,1,0:T(8,128)(2,1)} %get-tuple-element.198, f32[2,4,768]{2,1,0:T(4,128)S(1)} %neg.22, f32[2,4,768]{2,1,0:T(4,128)S(1)} %fusion.117, pred[768,768]{0,1:T(8,128)(4,1)S(1)} %iota_compare_fusion, bf16[1,768,2,5,64]{1,4,3,2,0:T(8,128)(2,1)S(1)} %get-tuple-element.146, ...), kind=kOutput, calls=%fused_computation.147 | convolution fusion | flops 1253769216 | bytes 31334400 | tf_op jit(solution)/shard_map/transpose(jvp(btgqh,bsgh->bgqts))/dot_general | solution.py:50
  378.8 9.6 %fusion.108 = bf16[1,768,2,1,128]{1,4,3,2,0:T(8,128)(2,1)S(1)} fusion(bf16[2,128,4,768]{3,1,2,0:T(8,128)(2,1)S(1)} %bitcast.301, f32[2,4,768]{2,1,0:T(4,128)S(1)} %fusion.117, f32[2,4,768]{2,1,0:T(4,128)S(1)} %get-tuple-element.195, f32[2,768,768,4]{2,1,3,0:T(8,128)} %get-tuple-element.196, pred[768,768]{0,1:T(8,128)(4,1)S(1)} %iota_compare_fusion), kind=kOutput, calls=%fused_computation.146 | convolution fusion | flops 1231749120 | bytes 21479424 | tf_op jit(solution)/shard_map/transpose(jvp(bgqts,bsgh->btgqh))/dot_general | solution.py:53
  394.2 13.2 %convolution_convert_fusion.1 = bf16[768,4096]{1,0:T(8,128)(2,1)} fusion(bf16[768,1536]{0,1:T(8,128)(2,1)} %bitcast.66, bf16[4096,1536]{0,1:T(8,128)(2,1)S(1)} %bitcast.291), kind=kOutput, calls=%fused_computation.50 | convolution fusion | flops 9666822144 | bytes 21233664 | tf_op jit(solution)/shard_map/tk,dk->td/dot_general | solution.py:69
  410.4 27.5 %collective-permute-done.7 = bf16[768,1024]{1,0:T(8,128)(2,1)} collective-permute-done((bf16[768,1024]{1,0:T(8,128)(2,1)}, bf16[768,1024]{1,0:T(8,128)(2,1)}, u32[]{:S(2)}, u32[]{:S(2)}) %collective-permute-start.7) | collective-permute-done | bytes 1572896 | tf_op jit(solution)/shard_map/ppermute | solution.py:57
  446.0 34.7 %convolution_convert_fusion = bf16[768,4096]{1,0:T(8,128)(2,1)} fusion(bf16[4096,4096]{1,0:T(8,128)(2,1)} %param.12, bf16[768,2048]{1,0:T(8,128)(2,1)} %multiply_convert_fusion, bf16[768,2048]{1,0:T(8,128)(2,1)} %multiply_convert_fusion.1), kind=kOutput, calls=%fused_computation.49 | convolution fusion | flops 25785532416 | bytes 46137344 | tf_op jit(solution)/shard_map/tf,df->td/dot_general | solution.py:69
  480.7 9.5 %fusion.86 = bf16[2,128,4,768]{3,1,2,0:T(8,128)(2,1)S(1)} fusion(bf16[1,768,2,6,128]{1,4,3,2,0:T(8,128)(2,1)} %copy-done.5, f32[2,4,768]{2,1,0:T(4,128)S(1)} %fusion.117, f32[2,4,768]{2,1,0:T(4,128)S(1)} %get-tuple-element.195, f32[2,768,768,4]{2,1,3,0:T(8,128)} %get-tuple-element.196, pred[768,768]{0,1:T(8,128)(4,1)S(1)} %iota_compare_fusion), kind=kOutput, calls=%fused_computation.127 | convolution fusion | flops 1232338944 | bytes 21479424 | tf_op jit(solution)/shard_map/jvp(bgqts,bsgh->btgqh)/dot_general | solution.py:53
  491.1 5.4 constant_dynamic-update-slice_fusion.3
  496.5 11.3 %collective-permute-done.19 = bf16[768,2048]{1,0:T(8,128)(2,1)} collective-permute-done((bf16[768,2048]{1,0:T(8,128)(2,1)}, bf16[768,2048]{1,0:T(8,128)(2,1)}, u32[]{:S(2)}, u32[]{:S(2)}) %collective-permute-start.19) | collective-permute-done | bytes 3145760 | tf_op jit(solution)/shard_map/ppermute | solution.py:57
  515.7 8.3 fusion.151
  534.2 4.0 constant_dynamic-update-slice_fusion.6
  538.1 4.0 constant_dynamic-update-slice_fusion.5
  542.7 4.0 constant_dynamic-update-slice_fusion.4
  546.7 52.2 %collective-permute-done.25 = bf16[768,2048]{1,0:T(8,128)(2,1)} collective-permute-done((bf16[768,2048]{1,0:T(8,128)(2,1)}, bf16[768,2048]{1,0:T(8,128)(2,1)}, u32[]{:S(2)}, u32[]{:S(2)}) %collective-permute-start.25) | collective-permute-done | bytes 3145760 | tf_op jit(solution)/shard_map/ppermute | solution.py:57
  600.5 12.0 %fusion.82 = f32[512,2048]{1,0:T(8,128)} fusion(bf16[3072,512]{1,0:T(8,128)(2,1)} %get-tuple-element.65, bf16[768,2048]{1,0:T(8,128)(2,1)} %collective-permute-done.17, bf16[768,2048]{1,0:T(8,128)(2,1)} %collective-permute-done.16, bf16[768,2048]{1,0:T(8,128)(2,1)} %collective-permute-done.15, bf16[768,2048]{1,0:T(8,128)(2,1)} %multiply_convert_fusion), kind=kOutput, calls=%fused_computation.118 | convolution fusion | flops 6492782592 | bytes 19922944 | tf_op jit(solution)/shard_map/tr,tc->rc/dot_general | solution.py:69
  612.4 11.2 %fusion.152 = f32[512,2048]{1,0:T(8,128)} fusion(bf16[3072,512]{1,0:T(8,128)(2,1)S(1)} %copy-done.17, bf16[3072,2048]{1,0:T(8,128)(2,1)} %constant_dynamic-update-slice_fusion.4), kind=kOutput, calls=%fused_computation.243 | convolution fusion | flops 6442450944 | bytes 19922944 | tf_op jit(solution)/shard_map/tr,tc->rc/dot_general | solution.py:69
  623.7 25.9 %collective-permute-done.22 = bf16[768,1536]{0,1:T(8,128)(2,1)} collective-permute-done((bf16[768,1536]{0,1:T(8,128)(2,1)}, bf16[768,1536]{0,1:T(8,128)(2,1)}, u32[]{:S(2)}, u32[]{:S(2)}) %collective-permute-start.22) | collective-permute-done | bytes 2359328 | tf_op jit(solution)/shard_map/ppermute | solution.py:57
  649.5 12.4 %fusion.79 = f32[512,2048]{1,0:T(8,128)} fusion(bf16[3072,512]{1,0:T(8,128)(2,1)} %get-tuple-element.65, bf16[768,2048]{1,0:T(8,128)(2,1)} %collective-permute-done.26, bf16[768,2048]{1,0:T(8,128)(2,1)} %collective-permute-done.25, bf16[768,2048]{1,0:T(8,128)(2,1)} %collective-permute-done.24, bf16[768,2048]{1,0:T(8,128)(2,1)} %multiply_convert_fusion.1), kind=kOutput, calls=%fused_computation.115 | convolution fusion | flops 6492782592 | bytes 19922944 | tf_op jit(solution)/shard_map/tr,tc->rc/dot_general | solution.py:69
  664.0 7.4 fusion.153
  671.5 7.5 fusion.154
  680.4 9.0 fusion.90
  689.5 11.3 %fusion.80 = f32[512,2048]{1,0:T(8,128)} fusion(bf16[3072,512]{1,0:T(8,128)(2,1)S(1)} %copy-done.26, bf16[768,2048]{1,0:T(8,128)(2,1)} %collective-permute-done.26, bf16[768,2048]{1,0:T(8,128)(2,1)} %collective-permute-done.25, bf16[768,2048]{1,0:T(8,128)(2,1)} %collective-permute-done.24, bf16[768,2048]{1,0:T(8,128)(2,1)} %multiply_convert_fusion.1), kind=kOutput, calls=%fused_computation.116 | convolution fusion | flops 6492782592 | bytes 19922944 | tf_op jit(solution)/shard_map/tr,tc->rc/dot_general | solution.py:69
  700.8 11.3 %fusion.81 = f32[512,2048]{1,0:T(8,128)} fusion(bf16[3072,512]{1,0:T(8,128)(2,1)S(1)} %copy-done.26, bf16[768,2048]{1,0:T(8,128)(2,1)} %collective-permute-done.17, bf16[768,2048]{1,0:T(8,128)(2,1)} %collective-permute-done.16, bf16[768,2048]{1,0:T(8,128)(2,1)} %collective-permute-done.15, bf16[768,2048]{1,0:T(8,128)(2,1)} %multiply_convert_fusion), kind=kOutput, calls=%fused_computation.117 | convolution fusion | flops 6492782592 | bytes 19922944 | tf_op jit(solution)/shard_map/tr,tc->rc/dot_general | solution.py:69
  712.1 11.8 %fusion.155 = f32[512,2048]{1,0:T(8,128)} fusion(bf16[3072,512]{1,0:T(8,128)(2,1)S(1)} %pad_maximum_fusion.7, bf16[3072,2048]{1,0:T(8,128)(2,1)} %copy-done), kind=kOutput, calls=%fused_computation.246 | convolution fusion | flops 6442450944 | bytes 19922944 | tf_op jit(solution)/shard_map/tr,tc->rc/dot_general | solution.py:69
  724.0 11.4 %fusion.156 = f32[512,2048]{1,0:T(8,128)} fusion(bf16[3072,512]{1,0:T(8,128)(2,1)S(1)} %pad_maximum_fusion.7, bf16[3072,2048]{1,0:T(8,128)(2,1)} %constant_dynamic-update-slice_fusion.4), kind=kOutput, calls=%fused_computation.247 | convolution fusion | flops 6442450944 | bytes 19922944 | tf_op jit(solution)/shard_map/tr,tc->rc/dot_general | solution.py:69
  741.1 9.0 fusion.89
  750.2 4.7 fusion.73
  759.8 4.9 collective-permute-done.28
  769.5 76.1 %collective-permute-done.35 = f32[512,2048]{1,0:T(8,128)} collective-permute-done((f32[512,2048]{1,0:T(8,128)}, f32[512,2048]{1,0:T(8,128)}, u32[]{:S(2)}, u32[]{:S(2)}) %collective-permute-start.35) | collective-permute-done | bytes 4194336 | tf_op jit(solution)/shard_map/ppermute | solution.py:57
  853.1 4.2 pad_maximum_fusion.3
  866.7 48.5 %collective-permute-done.31 = f32[4,4096]{1,0:T(4,128)S(1)} collective-permute-done((f32[4,4096]{1,0:T(4,128)S(1)}, f32[4,4096]{1,0:T(4,128)S(1)}, u32[]{:S(2)}, u32[]{:S(2)}) %collective-permute-start.31) | collective-permute-done | bytes 65568 | tf_op jit(solution)/shard_map/ppermute | solution.py:57
  916.7 3.9 pad_maximum_fusion.4
  921.3 4.1 add.368
  (308 shorter events, 137.2 us)
Async XLA Ops:
  7.2 120.5 %all-gather.5.cloned.1.call-start = ((), (), s32[]{:S(2)}) async-start(), calls=%async_computation.4 | async-start | bytes 7864320 | tf_op jit(solution)/shard_map/all_gather | solution.py:105
  7.9 234.8 %all-gather.7.cloned.1.call-start = ((), (), s32[]{:S(2)}) async-start(), calls=%async_computation.5 | async-start | bytes 7864320 | tf_op jit(solution)/shard_map/all_gather | solution.py:106
  8.7 741.4 %reduce-scatter.3.cloned.1.call-start = ((), (), s32[]{:S(2)}) async-start(), calls=%async_computation.2 | async-start | bytes 7864320 | tf_op jit(solution)/shard_map/reduce_scatter | solution.py:157
  9.4 133.8 %copy-start.33 = (f32[1,4096]{1,0:T(1,128)}, f32[1,4096]{1,0:T(1,128)S(1)}, u32[]{:S(2)}) copy-start(f32[1,4096]{1,0:T(1,128)S(1)} %get-tuple-element.181) | copy-start | bytes 49156
  9.4 185.2 %copy-start.35 = (f32[1,4096]{1,0:T(1,128)}, f32[1,4096]{1,0:T(1,128)S(1)}, u32[]{:S(2)}) copy-start(f32[1,4096]{1,0:T(1,128)S(1)} %get-tuple-element.179) | copy-start | bytes 49156
  42.1 168.4 %copy-start.28 = (f32[768,64]{0,1:T(8,128)}, f32[768,64]{0,1:T(8,128)S(1)}, u32[]{:S(2)}) copy-start(f32[768,64]{0,1:T(8,128)S(1)} %get-tuple-element.193) | copy-start | bytes 589828
  42.1 168.4 %copy-start.30 = (f32[768,64]{0,1:T(8,128)}, f32[768,64]{0,1:T(8,128)S(1)}, u32[]{:S(2)}) copy-start(f32[768,64]{0,1:T(8,128)S(1)} %get-tuple-element.194) | copy-start | bytes 589828
  134.7 165.0 %collective-permute-start.5 = (f32[768,2]{0,1:T(2,128)}, f32[768,2]{0,1:T(2,128)}, u32[]{:S(2)}, u32[]{:S(2)}) collective-permute-start(f32[768,2]{0,1:T(2,128)} %pad_maximum_fusion.31), channel_id=1, source_target_pairs={{0,3},{1,2},{2,1},{3,0},{4,7},{5,6},{6,5},{7,4},{8,11},{9,10},{10,... | collective-permute-start | bytes 18440 | tf_op jit(solution)/shard_map/ppermute | solution.py:57
  135.7 164.0 %collective-permute-start.4 = (f32[768,2]{0,1:T(2,128)}, f32[768,2]{0,1:T(2,128)}, u32[]{:S(2)}, u32[]{:S(2)}) collective-permute-start(f32[768,2]{0,1:T(2,128)} %pad_maximum_fusion.31), channel_id=1, source_target_pairs={{0,2},{1,3},{2,0},{3,1},{4,6},{5,7},{6,4},{7,5},{8,10},{9,11},{10,... | collective-permute-start | bytes 18440 | tf_op jit(solution)/shard_map/ppermute | solution.py:57
  136.3 165.0 %collective-permute-start.3 = (f32[768,2]{0,1:T(2,128)}, f32[768,2]{0,1:T(2,128)}, u32[]{:S(2)}, u32[]{:S(2)}) collective-permute-start(f32[768,2]{0,1:T(2,128)} %pad_maximum_fusion.31), channel_id=1, source_target_pairs={{0,1},{1,0},{2,3},{3,2},{4,5},{5,4},{6,7},{7,6},{8,9},{9,8},{10,11... | collective-permute-start | bytes 18440 | tf_op jit(solution)/shard_map/ppermute | solution.py:57
  140.0 162.2 %collective-permute-start.2 = (bf16[768,1024]{1,0:T(8,128)(2,1)}, bf16[768,1024]{1,0:T(8,128)(2,1)}, u32[]{:S(2)}, u32[]{:S(2)}) collective-permute-start(bf16[768,1024]{1,0:T(8,128)(2,1)} %pad_maximum_fusion.19), channel_id=1, source_target_pairs={{0,3},{1,2},{2,1},{3,0},{4,7},{5,6},{6,5},{7,4},{8,11},{9,10},{10,... | collective-permute-start | bytes 4718600 | tf_op jit(solution)/shard_map/ppermute | solution.py:57
  142.7 161.6 %collective-permute-start.1 = (bf16[768,1024]{1,0:T(8,128)(2,1)}, bf16[768,1024]{1,0:T(8,128)(2,1)}, u32[]{:S(2)}, u32[]{:S(2)}) collective-permute-start(bf16[768,1024]{1,0:T(8,128)(2,1)} %pad_maximum_fusion.18), channel_id=1, source_target_pairs={{0,2},{1,3},{2,0},{3,1},{4,6},{5,7},{6,4},{7,5},{8,10},{9,11},{10,... | collective-permute-start | bytes 4718600 | tf_op jit(solution)/shard_map/ppermute | solution.py:57
  299.7 208.2 %collective-permute-start.12 = (bf16[768,2048]{1,0:T(8,128)(2,1)}, bf16[768,2048]{1,0:T(8,128)(2,1)}, u32[]{:S(2)}, u32[]{:S(2)}) collective-permute-start(bf16[768,2048]{1,0:T(8,128)(2,1)} %get-tuple-element.64), channel_id=1, source_target_pairs={{0,1},{1,0},{2,3},{3,2},{4,5},{5,4},{6,7},{7,6},{8,9},{9,8},{10,11... | collective-permute-start | bytes 9437192 | tf_op jit(solution)/shard_map/ppermute | solution.py:57
  299.7 181.0 %collective-permute-start.13 = (bf16[768,2048]{1,0:T(8,128)(2,1)}, bf16[768,2048]{1,0:T(8,128)(2,1)}, u32[]{:S(2)}, u32[]{:S(2)}) collective-permute-start(bf16[768,2048]{1,0:T(8,128)(2,1)} %get-tuple-element.64), channel_id=1, source_target_pairs={{0,4},{1,5},{2,6},{3,7},{4,0},{5,1},{6,2},{7,3},{8,12},{9,13},{10,... | collective-permute-start | bytes 9437192 | tf_op jit(solution)/shard_map/ppermute | solution.py:57
  301.2 6.6 collective-permute-start
  302.2 105.3 %collective-permute-start.8 = (bf16[768,1024]{1,0:T(8,128)(2,1)}, bf16[768,1024]{1,0:T(8,128)(2,1)}, u32[]{:S(2)}, u32[]{:S(2)}) collective-permute-start(bf16[768,1024]{1,0:T(8,128)(2,1)} %pad_maximum_fusion.23), channel_id=1, source_target_pairs={{0,5},{1,4},{2,7},{3,6},{4,1},{5,0},{6,3},{7,2},{8,13},{9,12},{10,... | collective-permute-start | bytes 4718600 | tf_op jit(solution)/shard_map/ppermute | solution.py:57
  304.3 133.6 %collective-permute-start.7 = (bf16[768,1024]{1,0:T(8,128)(2,1)}, bf16[768,1024]{1,0:T(8,128)(2,1)}, u32[]{:S(2)}, u32[]{:S(2)}) collective-permute-start(bf16[768,1024]{1,0:T(8,128)(2,1)} %pad_maximum_fusion.22), channel_id=1, source_target_pairs={{0,4},{1,5},{2,6},{3,7},{4,0},{5,1},{6,2},{7,3},{8,12},{9,13},{10,... | collective-permute-start | bytes 4718600 | tf_op jit(solution)/shard_map/ppermute | solution.py:57
  307.8 134.0 %collective-permute-start.6 = (bf16[768,1024]{1,0:T(8,128)(2,1)}, bf16[768,1024]{1,0:T(8,128)(2,1)}, u32[]{:S(2)}, u32[]{:S(2)}) collective-permute-start(bf16[768,1024]{1,0:T(8,128)(2,1)} %pad_maximum_fusion.21), channel_id=1, source_target_pairs={{0,1},{1,0},{2,3},{3,2},{4,5},{5,4},{6,7},{7,6},{8,9},{9,8},{10,11... | collective-permute-start | bytes 4718600 | tf_op jit(solution)/shard_map/ppermute | solution.py:57
  407.5 107.0 %collective-permute-start.16 = (bf16[768,2048]{1,0:T(8,128)(2,1)}, bf16[768,2048]{1,0:T(8,128)(2,1)}, u32[]{:S(2)}, u32[]{:S(2)}) collective-permute-start(bf16[768,2048]{1,0:T(8,128)(2,1)} %multiply_convert_fusion), channel_id=1, source_target_pairs={{0,2},{1,3},{2,0},{3,1},{4,6},{5,7},{6,4},{7,5},{8,10},{9,11},{10,... | collective-permute-start | bytes 9437192 | tf_op jit(solution)/shard_map/ppermute | solution.py:57
  437.9 69.9 %collective-permute-start.19 = (bf16[768,2048]{1,0:T(8,128)(2,1)}, bf16[768,2048]{1,0:T(8,128)(2,1)}, u32[]{:S(2)}, u32[]{:S(2)}) collective-permute-start(bf16[768,2048]{1,0:T(8,128)(2,1)} %get-tuple-element.68), channel_id=1, source_target_pairs={{0,4},{1,5},{2,6},{3,7},{4,0},{5,1},{6,2},{7,3},{8,12},{9,13},{10,... | collective-permute-start | bytes 9437192 | tf_op jit(solution)/shard_map/ppermute | solution.py:57
  446.0 304.1 %reduce-scatter.5.cloned.1.call-start = ((), (), s32[]{:S(2)}) async-start(), calls=%async_computation.3 | async-start | bytes 7864320 | tf_op jit(solution)/shard_map/reduce_scatter | solution.py:169
  480.7 32.9 %collective-permute-start.14 = (bf16[768,2048]{1,0:T(8,128)(2,1)}, bf16[768,2048]{1,0:T(8,128)(2,1)S(1)}, u32[]{:S(2)}, u32[]{:S(2)}) collective-permute-start(bf16[768,2048]{1,0:T(8,128)(2,1)} %collective-permute-done.13), channel_id=1, source_target_pairs={{0,1},{1,0},{2,3},{3,2},{4,5},{5,4},{6,7},{7,6},{8,9},{9,8},{10,11... | collective-permute-start | bytes 9437192 | tf_op jit(solution)/shard_map/ppermute | solution.py:57
  490.3 43.3 %collective-permute-start.18 = (bf16[768,2048]{1,0:T(8,128)(2,1)}, bf16[768,2048]{1,0:T(8,128)(2,1)}, u32[]{:S(2)}, u32[]{:S(2)}) collective-permute-start(bf16[768,2048]{1,0:T(8,128)(2,1)} %get-tuple-element.68), channel_id=1, source_target_pairs={{0,1},{1,0},{2,3},{3,2},{4,5},{5,4},{6,7},{7,6},{8,9},{9,8},{10,11... | collective-permute-start | bytes 9437192 | tf_op jit(solution)/shard_map/ppermute | solution.py:57
  507.8 16.2 %collective-permute-start.11 = (bf16[768,256]{0,1:T(8,128)(2,1)S(1)}, bf16[768,256]{0,1:T(8,128)(2,1)S(1)}, u32[]{:S(2)}, u32[]{:S(2)}) collective-permute-start(bf16[768,256]{0,1:T(8,128)(2,1)S(1)} %pad_maximum_fusion.28), channel_id=1, source_target_pairs={{0,5},{1,4},{2,7},{3,6},{4,1},{5,0},{6,3},{7,2},{8,13},{9,12},{10,... | collective-permute-start | bytes 1179656 | tf_op jit(solution)/shard_map/ppermute | solution.py:57
  507.8 19.8 %collective-permute-start.10 = (bf16[768,256]{0,1:T(8,128)(2,1)S(1)}, bf16[768,256]{0,1:T(8,128)(2,1)S(1)}, u32[]{:S(2)}, u32[]{:S(2)}) collective-permute-start(bf16[768,256]{0,1:T(8,128)(2,1)S(1)} %pad_maximum_fusion.27), channel_id=1, source_target_pairs={{0,4},{1,5},{2,6},{3,7},{4,0},{5,1},{6,2},{7,3},{8,12},{9,13},{10,... | collective-permute-start | bytes 1179656 | tf_op jit(solution)/shard_map/ppermute | solution.py:57
  513.6 15.5 %collective-permute-start.9 = (bf16[768,256]{0,1:T(8,128)(2,1)S(1)}, bf16[768,256]{0,1:T(8,128)(2,1)S(1)}, u32[]{:S(2)}, u32[]{:S(2)}) collective-permute-start(bf16[768,256]{0,1:T(8,128)(2,1)S(1)} %pad_maximum_fusion.26), channel_id=1, source_target_pairs={{0,1},{1,0},{2,3},{3,2},{4,5},{5,4},{6,7},{7,6},{8,9},{9,8},{10,11... | collective-permute-start | bytes 1179656 | tf_op jit(solution)/shard_map/ppermute | solution.py:57
  514.5 27.7 %collective-permute-start.20 = (bf16[768,2048]{1,0:T(8,128)(2,1)}, bf16[768,2048]{1,0:T(8,128)(2,1)}, u32[]{:S(2)}, u32[]{:S(2)}) collective-permute-start(bf16[768,2048]{1,0:T(8,128)(2,1)} %collective-permute-done.19), channel_id=1, source_target_pairs={{0,1},{1,0},{2,3},{3,2},{4,5},{5,4},{6,7},{7,6},{8,9},{9,8},{10,11... | collective-permute-start | bytes 9437192 | tf_op jit(solution)/shard_map/ppermute | solution.py:57
  524.1 22.7 %collective-permute-start.15 = (bf16[768,2048]{1,0:T(8,128)(2,1)}, bf16[768,2048]{1,0:T(8,128)(2,1)}, u32[]{:S(2)}, u32[]{:S(2)}) collective-permute-start(bf16[768,2048]{1,0:T(8,128)(2,1)} %multiply_convert_fusion), channel_id=1, source_target_pairs={{0,1},{1,0},{2,3},{3,2},{4,5},{5,4},{6,7},{7,6},{8,9},{9,8},{10,11... | collective-permute-start | bytes 9437192 | tf_op jit(solution)/shard_map/ppermute | solution.py:57
  527.7 71.3 %collective-permute-start.25 = (bf16[768,2048]{1,0:T(8,128)(2,1)}, bf16[768,2048]{1,0:T(8,128)(2,1)}, u32[]{:S(2)}, u32[]{:S(2)}) collective-permute-start(bf16[768,2048]{1,0:T(8,128)(2,1)} %multiply_convert_fusion.1), channel_id=1, source_target_pairs={{0,2},{1,3},{2,0},{3,1},{4,6},{5,7},{6,4},{7,5},{8,10},{9,11},{10,... | collective-permute-start | bytes 9437192 | tf_op jit(solution)/shard_map/ppermute | solution.py:57
  529.2 69.8 %collective-permute-start.17 = (bf16[768,2048]{1,0:T(8,128)(2,1)}, bf16[768,2048]{1,0:T(8,128)(2,1)}, u32[]{:S(2)}, u32[]{:S(2)}) collective-permute-start(bf16[768,2048]{1,0:T(8,128)(2,1)} %collective-permute-done.16), channel_id=1, source_target_pairs={{0,1},{1,0},{2,3},{3,2},{4,5},{5,4},{6,7},{7,6},{8,9},{9,8},{10,11... | collective-permute-start | bytes 9437192 | tf_op jit(solution)/shard_map/ppermute | solution.py:57
  533.6 115.9 %collective-permute-start.24 = (bf16[768,2048]{1,0:T(8,128)(2,1)}, bf16[768,2048]{1,0:T(8,128)(2,1)}, u32[]{:S(2)}, u32[]{:S(2)}) collective-permute-start(bf16[768,2048]{1,0:T(8,128)(2,1)} %multiply_convert_fusion.1), channel_id=1, source_target_pairs={{0,1},{1,0},{2,3},{3,2},{4,5},{5,4},{6,7},{7,6},{8,9},{9,8},{10,11... | collective-permute-start | bytes 9437192 | tf_op jit(solution)/shard_map/ppermute | solution.py:57
  542.2 107.4 %collective-permute-start.22 = (bf16[768,1536]{0,1:T(8,128)(2,1)}, bf16[768,1536]{0,1:T(8,128)(2,1)}, u32[]{:S(2)}, u32[]{:S(2)}) collective-permute-start(bf16[768,1536]{0,1:T(8,128)(2,1)} %bitcast.66), channel_id=1, source_target_pairs={{0,2},{1,3},{2,0},{3,1},{4,6},{5,7},{6,4},{7,5},{8,10},{9,11},{10,... | collective-permute-start | bytes 7077896 | tf_op jit(solution)/shard_map/ppermute | solution.py:57
  546.7 132.2 %collective-permute-start.21 = (bf16[768,1536]{0,1:T(8,128)(2,1)}, bf16[768,1536]{0,1:T(8,128)(2,1)}, u32[]{:S(2)}, u32[]{:S(2)}) collective-permute-start(bf16[768,1536]{0,1:T(8,128)(2,1)} %bitcast.66), channel_id=1, source_target_pairs={{0,1},{1,0},{2,3},{3,2},{4,5},{5,4},{6,7},{7,6},{8,9},{9,8},{10,11... | collective-permute-start | bytes 7077896 | tf_op jit(solution)/shard_map/ppermute | solution.py:57
  599.0 50.6 %collective-permute-start.26 = (bf16[768,2048]{1,0:T(8,128)(2,1)}, bf16[768,2048]{1,0:T(8,128)(2,1)}, u32[]{:S(2)}, u32[]{:S(2)}) collective-permute-start(bf16[768,2048]{1,0:T(8,128)(2,1)} %collective-permute-done.25), channel_id=1, source_target_pairs={{0,1},{1,0},{2,3},{3,2},{4,5},{5,4},{6,7},{7,6},{8,9},{9,8},{10,11... | collective-permute-start | bytes 9437192 | tf_op jit(solution)/shard_map/ppermute | solution.py:57
  599.0 262.1 %collective-permute-start.36 = (f32[512,2048]{1,0:T(8,128)}, f32[512,2048]{1,0:T(8,128)}, u32[]{:S(2)}, u32[]{:S(2)}) collective-permute-start(f32[512,2048]{1,0:T(8,128)} %fusion.151), channel_id=1, source_target_pairs={{0,2},{1,3},{2,0},{3,1},{4,6},{5,7},{6,4},{7,5},{8,10},{9,11},{10,... | collective-permute-start | bytes 12582920 | tf_op jit(solution)/shard_map/ppermute | solution.py:57
  649.5 30.9 %collective-permute-start.23 = (bf16[768,1536]{0,1:T(8,128)(2,1)}, bf16[768,1536]{0,1:T(8,128)(2,1)}, u32[]{:S(2)}, u32[]{:S(2)}) collective-permute-start(bf16[768,1536]{0,1:T(8,128)(2,1)} %collective-permute-done.22), channel_id=1, source_target_pairs={{0,1},{1,0},{2,3},{3,2},{4,5},{5,4},{6,7},{7,6},{8,9},{9,8},{10,11... | collective-permute-start | bytes 7077896 | tf_op jit(solution)/shard_map/ppermute | solution.py:57
  661.9 188.1 %collective-permute-start.34 = (f32[512,2048]{1,0:T(8,128)}, f32[512,2048]{1,0:T(8,128)}, u32[]{:S(2)}, u32[]{:S(2)}) collective-permute-start(f32[512,2048]{1,0:T(8,128)} %fusion.79), channel_id=1, source_target_pairs={{0,4},{1,5},{2,6},{3,7},{4,0},{5,1},{6,2},{7,3},{8,12},{9,13},{10,... | collective-permute-start | bytes 12582920 | tf_op jit(solution)/shard_map/ppermute | solution.py:57
  662.0 183.6 %collective-permute-start.35 = (f32[512,2048]{1,0:T(8,128)}, f32[512,2048]{1,0:T(8,128)}, u32[]{:S(2)}, u32[]{:S(2)}) collective-permute-start(f32[512,2048]{1,0:T(8,128)} %fusion.82), channel_id=1, source_target_pairs={{0,4},{1,5},{2,6},{3,7},{4,0},{5,1},{6,2},{7,3},{8,12},{9,13},{10,... | collective-permute-start | bytes 12582920 | tf_op jit(solution)/shard_map/ppermute | solution.py:57
  679.0 178.3 %collective-permute-start.37 = (f32[512,2048]{1,0:T(8,128)}, f32[512,2048]{1,0:T(8,128)}, u32[]{:S(2)}, u32[]{:S(2)}) collective-permute-start(f32[512,2048]{1,0:T(8,128)} %fusion.152), channel_id=1, source_target_pairs={{0,2},{1,3},{2,0},{3,1},{4,6},{5,7},{6,4},{7,5},{8,10},{9,11},{10,... | collective-permute-start | bytes 12582920 | tf_op jit(solution)/shard_map/ppermute | solution.py:57
  755.0 4.3 collective-permute-start.27
  759.4 5.4 collective-permute-start.28
  764.8 1.3 collective-permute-start.29
  766.1 155.2 %collective-permute-start.33 = (f32[512,1536]{1,0:T(8,128)}, f32[512,1536]{1,0:T(8,128)}, u32[]{:S(2)}, u32[]{:S(2)}) collective-permute-start(f32[512,1536]{1,0:T(8,128)} %fusion.90), channel_id=1, source_target_pairs={{0,4},{1,5},{2,6},{3,7},{4,0},{5,1},{6,2},{7,3},{8,12},{9,13},{10,... | collective-permute-start | bytes 9437192 | tf_op jit(solution)/shard_map/ppermute | solution.py:57
  845.6 85.6 %collective-permute-start.39 = (f32[128,2048]{1,0:T(8,128)}, f32[128,2048]{1,0:T(8,128)}, u32[]{:S(2)}, u32[]{:S(2)}) collective-permute-start(f32[128,2048]{1,0:T(8,128)} %fusion.154), channel_id=1, source_target_pairs={{0,2},{1,3},{2,0},{3,1},{4,6},{5,7},{6,4},{7,5},{8,10},{9,11},{10,... | collective-permute-start | bytes 3145736 | tf_op jit(solution)/shard_map/ppermute | solution.py:57
  850.1 65.2 %collective-permute-start.31 = (f32[4,4096]{1,0:T(4,128)S(1)}, f32[4,4096]{1,0:T(4,128)S(1)}, u32[]{:S(2)}, u32[]{:S(2)}) collective-permute-start(f32[4,4096]{1,0:T(4,128)S(1)} %add.364), channel_id=1, source_target_pairs={{0,4},{1,5},{2,6},{3,7},{4,0},{5,1},{6,2},{7,3},{8,12},{9,13},{10,... | collective-permute-start | bytes 196616 | tf_op jit(solution)/shard_map/ppermute | solution.py:57
  857.3 75.6 %collective-permute-start.38 = (f32[128,2048]{1,0:T(8,128)}, f32[128,2048]{1,0:T(8,128)}, u32[]{:S(2)}, u32[]{:S(2)}) collective-permute-start(f32[128,2048]{1,0:T(8,128)} %fusion.153), channel_id=1, source_target_pairs={{0,2},{1,3},{2,0},{3,1},{4,6},{5,7},{6,4},{7,5},{8,10},{9,11},{10,... | collective-permute-start | bytes 3145736 | tf_op jit(solution)/shard_map/ppermute | solution.py:57
  861.1 59.6 %collective-permute-start.32 = (f32[4,4096]{1,0:T(4,128)S(1)}, f32[4,4096]{1,0:T(4,128)S(1)}, u32[]{:S(2)}, u32[]{:S(2)}) collective-permute-start(f32[4,4096]{1,0:T(4,128)S(1)} %add.364), channel_id=1, source_target_pairs={{0,6},{1,7},{2,4},{3,5},{4,2},{5,3},{6,0},{7,1},{8,14},{9,15},{10,... | collective-permute-start | bytes 196616 | tf_op jit(solution)/shard_map/ppermute | solution.py:57
  915.2 5.4 collective-permute-start.30
  (65 other events, 820.5 us)
Sparse Core Ops, SparseCore 0:
  9.6 118.0 all-gather.4
  129.2 113.5 all-gather.6
  446.1 108.0 reduce-scatter.2
  556.9 111.2 reduce-scatter.4
